TPU v7x, 256 devices: a 4x2x16 block of a 4x16x16 slice. The times are simulated.
256 devices in a mesh: rep: 2 (over y), gx: 128 (over x, z, core).
Axes of the slice: x: 4, y: 2, z: 16, core: 2. Of those that a mesh axis runs over, the one named last changes fastest.
The devices are a block of a 4x16x16 slice.
Arguments:
- positions: float32 [3, 262144], P(None, ('rep', 'gx')), parts along dimension 1, may hold values from 0 to 8, as said below
- field: float32 [3, 262144], P(None, ('rep', 'gx')), parts along dimension 1, may hold values from -45 to 45
- inv_polar: float32 [262144], P(('rep', 'gx')), parts along dimension 0, may hold values from 2 to 8
- x_spline: float32 [2, 5, 262144], P(None, None, ('rep', 'gx')), parts along dimension 2, may hold values from -1 to 1, as said below
- yz_spline: float32 [4, 262144, 128], P(None, ('rep', 'gx')), parts along dimension 1, may hold values from -1 to 1, as said below
- tile_list: int32 [2048, 7], P(('rep', 'gx')), parts along dimension 0, may hold values from 0 to 13, as said below
- tile_count: int32 [2048], P(('rep', 'gx')), parts along dimension 0, may hold values from 1 to 7, as said below
Outputs:
- dipoles: float32 [3, 262144], P(None, ('rep', 'gx')), parts along dimension 1
- residual: float32 [3, 262144], P(None, ('rep', 'gx')), parts along dimension 1
There are 2 independent parts, one for each index of `rep`. A program takes and returns all parts, laid end to end along the dimension named above; each array names one. Nothing has to cross between parts.
Inputs may be any that keep to these rules, and one draw needn't show every extreme that they name: `positions`: the first coordinate of an atom of block b of its slab lies in [b, b + 1); the other two lie in [0, 2). x_spline[0, k, i] and x_spline[1, k, i] are the cardinal B-spline of order 5 and its derivative at u_i + 4 - k for some u_i in [0, 1). `yz_spline`: rows 0 and 1 hold, for each atom, the cardinal B-spline of order 5 and its derivative at u + 4 - k placed at grid line (t + k) mod 128 for k < 5, for some start t and some u in [0, 1), and zero elsewhere; rows 2 and 3 likewise with their own start and offset. `tile_list`: row g = s * 8 + b lists in rising order the extended blocks b + 3 + e, -3 <= e <= 3, for which global blocks g and g + e (modulo 1024) are neighbours; being neighbours is symmetric and always holds for e = 0; entries from tile_count[g] on equal b + 3. `tile_count`: global block 0 has all 7 neighbours.
All inputs are finite; a program needn't handle non-finite values.
Results may differ from a plain program's by a relative error of at most 0.0003.
Values sent between devices are 32-bit elements; how exact they have to be, the bound alone decides.
A program may use at most 64 MiB of HBM per device.

v0:
```python
import jax
import jax.numpy as jnp
from jax import lax
from jax.sharding import Mesh
from jax.sharding import PartitionSpec as P

GRID = 128
ORDER = 5
TILE = 128
HALO_BLK = 3
ITERS = 3
GX = ("gx_0", "gx_1", "gx_2")
REP_GX = ("rep", "gx_0", "gx_1", "gx_2")


PAIR_C = 0.025
RECIP_C = 8192.0
DAMP = 0.0008
EXACT = lax.Precision.HIGHEST


def from_behind(x, axis, by):
    devices = lax.axis_size(axis)
    return lax.ppermute(x, axis, [(i, (i + by) % devices) for i in range(devices)])


def extended(x, sides, width):
    for axis, dim in sides:
        devices, length = (lax.axis_size(axis), x.shape[dim])
        up = [(i, (i + 1) % devices) for i in range(devices)]
        down = [(j, i) for i, j in up]
        last = lax.slice_in_dim(x, length - width, length, axis=dim)
        first = lax.slice_in_dim(x, 0, width, axis=dim)
        before = lax.ppermute(last, axis, up)
        after = lax.ppermute(first, axis, down)
        x = jnp.concatenate([before, x, after], axis=dim)
    return x


def split_up(x, dim, devices):
    before, after = (x.shape[:dim], x.shape[dim + 1 :])
    return jnp.moveaxis(x.reshape(*before, devices, -1, *after), dim, 0)


def in_order(tiles, dim):
    dims = list(tiles.shape[1:])
    dims[dim] *= tiles.shape[0]
    return jnp.moveaxis(tiles, 0, dim).reshape(dims)


def turned_blocks(tiles, axes, sequence):
    dims = [lax.axis_size(a) for a in axes]
    tiles = tiles.reshape(*dims, *tiles.shape[1:])
    for k in sequence:
        tiles = lax.all_to_all(tiles, axes[k], split_axis=k, concat_axis=k, tiled=True)
    return tiles.reshape(-1, *tiles.shape[len(axes) :])


def exchange_by_chip(x, groups, sequence, split_dim, concat_dim):
    devices = lax.axis_size(groups[0]) * lax.axis_size(groups[1])
    tiles = split_up(x, split_dim, devices)
    return in_order(turned_blocks(tiles, groups, sequence), concat_dim)


def over_axes(x, axes):
    for axis in axes:
        x = lax.psum(x, axis)
    return x


def pair_field(home_pos, ext_pos, ext_vec, tile_rows, live_counts):
    slab_blocks = home_pos.shape[1] // TILE
    ext_blocks = ext_pos.shape[1] // TILE
    home_blocks = home_pos.reshape(3, slab_blocks, TILE).transpose(1, 0, 2)
    pos_blocks = ext_pos.reshape(3, ext_blocks, TILE)
    vec_blocks = ext_vec.reshape(3, ext_blocks, TILE)
    slot_index = jnp.arange(tile_rows.shape[1], dtype=jnp.int32)
    self_pair = jnp.eye(TILE, dtype=bool)

    def one_block(carried, scan_item):
        home_block, tile_row, live_count, block_index = scan_item
        near_pos = jnp.take(pos_blocks, tile_row, axis=1)
        near_vec = jnp.take(vec_blocks, tile_row, axis=1)
        offsets = home_block[:, None, :, None] - near_pos[:, :, None, :]
        distance_sq = jnp.sum(offsets * offsets, axis=0) + 1.0
        inverse = lax.rsqrt(distance_sq)
        third_power = inverse * inverse * inverse
        fifth_power = third_power * inverse * inverse
        same_block = (tile_row == block_index + HALO_BLK)[:, None, None]
        live_mask = (slot_index < live_count)[:, None, None] & ~(same_block & self_pair[None])
        third_power = jnp.where(live_mask, third_power, 0.0)
        fifth_power = jnp.where(live_mask, fifth_power, 0.0)
        projection = jnp.sum(offsets * near_vec[:, :, None, :], axis=0)
        field_sum = jnp.sum(
            third_power[None] * near_vec[:, :, None, :]
            - 3.0 * (fifth_power * projection)[None] * offsets,
            axis=(1, 3),
        )
        return (carried, PAIR_C * field_sum)

    block_ids = jnp.arange(slab_blocks, dtype=jnp.int32)
    unused_carry, blocks_out = lax.scan(
        one_block, jnp.zeros((), jnp.float32), (home_blocks, tile_rows, live_counts, block_ids)
    )
    return blocks_out.transpose(1, 0, 2).reshape(3, slab_blocks * TILE)


def slab_weights(local_plane, x_spline, planes):
    spline_steps = jnp.arange(ORDER, dtype=jnp.int32)
    plane_index = jnp.arange(planes, dtype=jnp.int32)
    matches = local_plane[None, :, None] + spline_steps[:, None, None] == plane_index[None, None, :]
    spline_value = jnp.sum(jnp.where(matches, x_spline[0][:, :, None], 0.0), axis=0)
    spline_slope = jnp.sum(jnp.where(matches, x_spline[1][:, :, None], 0.0), axis=0)
    return (spline_value, spline_slope)


def spread_dipoles(vector, spline_value, spline_slope, yz_spline):
    atoms_here = spline_value.shape[0]
    planes = spline_value.shape[1]
    grid_lines = yz_spline.shape[2]
    lead_terms = (vector[0][:, None] * spline_slope)[:, :, None] * yz_spline[0][:, None, :]
    lead_terms = (
        lead_terms + (vector[1][:, None] * spline_value)[:, :, None] * yz_spline[1][:, None, :]
    )
    tail_terms = (vector[2][:, None] * spline_value)[:, :, None] * yz_spline[0][:, None, :]
    contract = (((0,), (0,)), ((), ()))
    charge = lax.dot_general(
        lead_terms.reshape(atoms_here, planes * grid_lines), yz_spline[2], contract, precision=EXACT
    )
    charge = charge + lax.dot_general(
        tail_terms.reshape(atoms_here, planes * grid_lines), yz_spline[3], contract, precision=EXACT
    )
    return charge.reshape(planes, grid_lines, grid_lines)


def gather_field(potential, spline_value, spline_slope, yz_spline):
    planes = potential.shape[0]
    grid_lines = potential.shape[1]
    atoms_here = spline_value.shape[0]
    flat_grid = potential.reshape(planes * grid_lines, grid_lines)
    contract = (((1,), (1,)), ((), ()))
    plain_sum = lax.dot_general(yz_spline[2], flat_grid, contract, precision=EXACT).reshape(
        atoms_here, planes, grid_lines
    )
    tilted_sum = lax.dot_general(yz_spline[3], flat_grid, contract, precision=EXACT).reshape(
        atoms_here, planes, grid_lines
    )
    first_comp = jnp.sum(
        spline_slope[:, :, None] * yz_spline[0][:, None, :] * plain_sum, axis=(1, 2)
    )
    second_comp = jnp.sum(
        spline_value[:, :, None] * yz_spline[1][:, None, :] * plain_sum, axis=(1, 2)
    )
    third_comp = jnp.sum(
        spline_value[:, :, None] * yz_spline[0][:, None, :] * tilted_sum, axis=(1, 2)
    )
    return jnp.stack([first_comp, second_comp, third_comp])


def mode_of(freq, size):
    half_size = size // 2
    mode_num = jnp.where(freq <= half_size, freq, freq - half_size)
    weight = jnp.where((freq == 0) | (freq == half_size), 1.0 / size, 2.0 / size)
    return (mode_num.astype(jnp.float32), weight.astype(jnp.float32))


def basis_rows(size, points):
    freq = jnp.arange(size, dtype=jnp.int32)
    half_size = size // 2
    mode_num = jnp.where(freq <= half_size, freq, freq - half_size)
    phase = mode_num[:, None] * points[None, :] % size
    angle = phase.astype(jnp.float32) * (2.0 * jnp.pi / size)
    return jnp.where((freq <= half_size)[:, None], jnp.cos(angle), jnp.sin(angle))


def kernel_block(x_modes, x_weights, y_modes, y_weights, z_modes, z_weights):
    mode_sq = (
        x_modes[:, None, None] * x_modes[:, None, None]
        + y_modes[None, :, None] * y_modes[None, :, None]
        + z_modes[None, None, :] * z_modes[None, None, :]
    )
    safe_sq = jnp.where(mode_sq > 0, mode_sq, 1.0)
    green = jnp.where(mode_sq > 0, RECIP_C * jnp.exp(-DAMP * safe_sq) / safe_sq, 0.0)
    return green * x_weights[:, None, None] * y_weights[None, :, None] * z_weights[None, None, :]


def forward_lines(charge, fourier_rows):
    along_z = jnp.einsum("pyz,kz->pyk", charge, fourier_rows, precision=EXACT)
    return jnp.einsum("jy,pyk->pjk", fourier_rows, along_z, precision=EXACT)


def inverse_lines(spectrum, fourier_rows):
    along_z = jnp.einsum("pjk,kz->pjz", spectrum, fourier_rows, precision=EXACT)
    return jnp.einsum("jy,pjz->pyz", fourier_rows, along_z, precision=EXACT)


def from_above(piece, distance):
    return from_behind(piece, GX, -distance)


def from_below(piece, distance):
    return from_behind(piece, GX, distance)


def per_device(positions, field, inv_polar, x_spline, yz_spline, tile_list, tile_count):
    rank_count = lax.axis_size(GX)
    rank_index = lax.axis_index(GX)
    atoms_here = positions.shape[1]
    planes = GRID // rank_count
    extent = planes + 4
    halo_atoms = HALO_BLK * TILE
    slab_blocks = atoms_here // TILE
    local_plane = jnp.arange(atoms_here, dtype=jnp.int32) * planes // atoms_here
    spline_value, spline_slope = slab_weights(local_plane, x_spline, extent)
    ext_pos = extended(positions, ((GX, 1),), halo_atoms)
    shift_x = jnp.concatenate(
        [
            jnp.full((halo_atoms,), -1.0 * slab_blocks, jnp.float32),
            jnp.zeros((atoms_here,), jnp.float32),
            jnp.full((halo_atoms,), 1.0 * slab_blocks, jnp.float32),
        ]
    )
    ext_pos = ext_pos.at[0].add(shift_x)
    fourier_rows = basis_rows(GRID, jnp.arange(GRID, dtype=jnp.int32))
    ky_count = GRID // rank_count
    all_freq = jnp.arange(GRID, dtype=jnp.int32)
    ky_freq = rank_index * ky_count + jnp.arange(ky_count, dtype=jnp.int32)
    full_modes, full_weights = mode_of(all_freq, GRID)
    ky_modes, ky_weights = mode_of(ky_freq, GRID)
    kernel = kernel_block(full_modes, full_weights, ky_modes, ky_weights, full_modes, full_weights)
    kernel = kernel.reshape(GRID, ky_count * GRID)

    def reciprocal(charge):
        rim_planes = min(2, planes)
        hop_count = (planes + 1) // planes
        owned_planes = charge[2 : 2 + planes]
        for distance in range(1, hop_count + 1):
            lower_piece = charge[2 - distance * rim_planes : 2 - (distance - 1) * rim_planes]
            owned_planes = owned_planes.at[planes - rim_planes :].add(
                from_above(lower_piece, distance)
            )
            upper_piece = charge[
                planes + 2 + (distance - 1) * rim_planes : planes + 2 + distance * rim_planes
            ]
            owned_planes = owned_planes.at[:rim_planes].add(from_below(upper_piece, distance))
        spectrum = forward_lines(owned_planes, fourier_rows)
        pencils = exchange_by_chip(spectrum, (("gx_0", "gx_1"), "gx_2"), (1, 0), 1, 0)
        flat_pencils = pencils.reshape(GRID, ky_count * GRID)
        spectral_lines = jnp.dot(fourier_rows, flat_pencils, precision=EXACT) * kernel
        returned_lines = lax.dot_general(
            fourier_rows, spectral_lines, (((0,), (0,)), ((), ())), precision=EXACT
        )
        returned = exchange_by_chip(
            returned_lines.reshape(GRID, ky_count, GRID), (("gx_0", "gx_1"), "gx_2"), (1, 0), 0, 1
        )
        own_potential = inverse_lines(returned, fourier_rows)
        below_parts = [from_below(own_potential, distance) for distance in range(hop_count, 0, -1)]
        above_parts = [from_above(own_potential, distance) for distance in range(1, hop_count + 1)]
        return jnp.concatenate(below_parts + [own_potential] + above_parts, axis=0)

    def apply(vector):
        ext_vec = extended(vector, ((GX, 1),), halo_atoms)
        near_field = pair_field(positions, ext_pos, ext_vec, tile_list, tile_count)
        charge = spread_dipoles(vector, spline_value, spline_slope, yz_spline)
        far_field = gather_field(reciprocal(charge), spline_value, spline_slope, yz_spline)
        return inv_polar[None, :] * vector + far_field - near_field

    def paired(residual, precond, applied):
        return (
            over_axes(jnp.sum(residual * precond), GX),
            over_axes(jnp.sum(applied * precond), GX),
        )

    dipoles = jnp.zeros_like(field)
    residual = field
    precond = field / inv_polar[None, :]
    applied = apply(precond)
    rz_now, curvature = paired(residual, precond, applied)
    step_size = rz_now / curvature
    direction = precond
    applied_dir = applied
    for sweep_index in range(ITERS):
        dipoles = dipoles + step_size * direction
        residual = residual - step_size * applied_dir
        if sweep_index + 1 < ITERS:
            precond = residual / inv_polar[None, :]
            applied = apply(precond)
            rz_next, curvature = paired(residual, precond, applied)
            beta_ratio = rz_next / rz_now
            step_size = rz_next / (curvature - beta_ratio * rz_next / step_size)
            direction = precond + beta_ratio * direction
            applied_dir = applied + beta_ratio * applied_dir
            rz_now = rz_next
    return (dipoles, residual)


def solution(mesh):
    torus = Mesh(mesh.devices.reshape(mesh.shape["rep"], 4, 16, 2), ("rep", "gx_0", "gx_1", "gx_2"))
    in_specs = (
        P(None, REP_GX),
        P(None, REP_GX),
        P(REP_GX),
        P(None, None, REP_GX),
        P(None, REP_GX, None),
        P(REP_GX, None),
        P(REP_GX),
    )
    out_specs = (P(None, REP_GX), P(None, REP_GX))
    return jax.shard_map(
        per_device, mesh=torus, in_specs=in_specs, out_specs=out_specs, check_vma=False
    )
```

profile of v0, /device:TPU:33, one launch (start us, length us, event | category | flops | bytes accessed | tf_op | source)
XLA Modules:
  0.0 596.1 jit_solution(14503698682587773255)
XLA Ops:
  5.5 5.2 broadcast_multiply_fusion.3
  10.8 2.2 fusion.64
  13.0 2.2 convolution_add_fusion.2
  15.9 20.4 %collective-permute-start = (f32[1,128,128]{2,1,0:T(8,128)}, f32[1,128,128]{2,1,0:T(8,128)}, u32[]{:S(2)}, u32[]{:S(2)}) collective-permute-start(f32[1,128,128]{2,1,0:T(8,128)} %get-tuple-element.678), channel_id=1, source_target_pairs={{0,127},{1,0},{2,1},{3,2},{4,3},{5,4},{6,5},{7,6},{8,7},{9,8},{10,... | collective-permute-start | bytes 196616 | tf_op jit(solution)/shard_map/ppermute | solution.py:24
  36.4 10.2 %collective-permute-start.2 = (f32[1,128,128]{2,1,0:T(8,128)}, f32[1,128,128]{2,1,0:T(8,128)}, u32[]{:S(2)}, u32[]{:S(2)}) collective-permute-start(f32[1,128,128]{2,1,0:T(8,128)} %get-tuple-element.680), channel_id=1, source_target_pairs={{0,126},{1,127},{2,0},{3,1},{4,2},{5,3},{6,4},{7,5},{8,6},{9,7},{1... | collective-permute-start | bytes 196616 | tf_op jit(solution)/shard_map/ppermute | solution.py:24
  52.5 3.8 collective-permute-start.11
  56.2 1.5 fusion.102
  59.1 8.5 %all_to_all.60 = f32[64,2,1,1,128]{4,0,3,2,1:T(8,128)S(1)} all-to-all(f32[64,2,1,1,128]{4,0,3,2,1:T(8,128)S(1)} %copy.68), channel_id=1, replica_groups=mesh['rep'=2,'gx_0'=4,'gx_1'=16,'gx_2'=2] {'gx_2'}, dimensions={1} | all-to-all | bytes 131072 | tf_op jit(solution)/shard_map/all_to_all | solution.py:55
  68.2 6.5 %all-to-all-start.1 = ((f32[64,2,1,1,128]{4,1,3,2,0:T(2,128)}), f32[64,2,1,1,128]{4,1,3,2,0:T(2,128)S(1)}, u32[]{:S(2)}, u32[]{:S(2)}) async-start(f32[64,2,1,1,128]{4,1,3,2,0:T(2,128)} %copy.69), calls=%async_computation.1 | async-start | bytes 131072 | tf_op jit(solution)/shard_map/all_to_all | solution.py:55
  76.1 10.7 %all-to-all-done.1 = f32[64,2,1,1,128]{4,1,3,2,0:T(2,128)S(1)} async-done(((f32[64,2,1,1,128]{4,1,3,2,0:T(2,128)}), f32[64,2,1,1,128]{4,1,3,2,0:T(2,128)S(1)}, u32[]{:S(2)}, u32[]{:S(2)}) %all-to-all-start.1) | async-done | bytes 65568 | tf_op jit(solution)/shard_map/all_to_all | solution.py:55
  89.4 5.4 all_to_all.61
  95.5 6.5 %all-to-all-start.3 = ((f32[64,2,1,1,128]{4,1,3,2,0:T(2,128)}), f32[64,2,1,1,128]{4,1,3,2,0:T(2,128)S(1)}, u32[]{:S(2)}, u32[]{:S(2)}) async-start(f32[64,2,1,1,128]{4,1,3,2,0:T(2,128)} %copy.71), calls=%async_computation.3 | async-start | bytes 131072 | tf_op jit(solution)/shard_map/all_to_all | solution.py:55
  103.5 10.6 %all-to-all-done.3 = f32[64,2,1,1,128]{4,1,3,2,0:T(2,128)S(1)} async-done(((f32[64,2,1,1,128]{4,1,3,2,0:T(2,128)}), f32[64,2,1,1,128]{4,1,3,2,0:T(2,128)S(1)}, u32[]{:S(2)}, u32[]{:S(2)}) %all-to-all-start.3) | async-done | bytes 65568 | tf_op jit(solution)/shard_map/all_to_all | solution.py:55
  115.8 43.6 %while.58 = (s32[]{:T(128)}, f32[8,3,128]{2,1,0:T(4,128)S(1)}, s32[8]{0:T(128)S(1)}, s32[8,7]{1,0:T(8,128)}, s32[8]{0:T(128)S(1)}, /*index=5*/f32[8,3,128]{2,1,0...) while((s32[]{:T(128)}, f32[8,3,128]{2,1,0:T(4,128)S(1)}, ...), condition=%wide.region_13.15_spmd.clone, body=%wide.region_9.14_spmd.clone.sunk | while | flops 4610363 | bytes 3891027 | solution.py:102
  159.5 2.8 collective-permute-start.5
  162.3 4.7 collective-permute-start.7
  167.1 1.7 collective-permute-done.7
  168.7 3.3 fusion.45
  172.1 4.3 fusion.47
  177.1 6.7 %all-reduce.5 = (f32[]{:T(128)}, f32[]{:T(128)}) all-reduce(f32[]{:T(128)} %get-tuple-element.562, f32[]{:T(128)} %get-tuple-element.561), channel_id=1, replica_groups=mesh['rep'=2,'gx_0'=4,'gx_1'=16,'gx_2'=2] {'gx_0'}, use_global_device_ids=true, to_apply=%region_1.2 | all-reduce | flops 2 | bytes 16 | tf_op jit(solution)/shard_map/psum | solution.py:67
  183.7 26.3 %all-reduce.2 = (f32[]{:T(128)}, f32[]{:T(128)}) all-reduce(f32[]{:T(128)} %get-tuple-element.621, f32[]{:T(128)} %get-tuple-element.622), channel_id=1, replica_groups=mesh['rep'=2,'gx_0'=4,'gx_1'=16,'gx_2'=2] {'gx_1'}, use_global_device_ids=true, to_apply=%region_2.3 | all-reduce | flops 2 | bytes 16 | tf_op jit(solution)/shard_map/psum | solution.py:67
  210.1 14.0 %all-reduce.8 = (f32[]{:T(128)}, f32[]{:T(128)}) all-reduce(f32[]{:T(128)} %get-tuple-element.615, f32[]{:T(128)} %get-tuple-element.616), channel_id=1, replica_groups=mesh['rep'=2,'gx_0'=4,'gx_1'=16,'gx_2'=2] {'gx_2'}, use_global_device_ids=true, to_apply=%region_3.4 | all-reduce | flops 2 | bytes 16 | tf_op jit(solution)/shard_map/psum | solution.py:67
  225.5 1.9 broadcast_multiply_fusion.1
  227.4 2.2 fusion.60
  229.7 2.2 convolution_add_fusion.1
  232.4 1.6 collective-permute-start.13
  234.0 3.4 collective-permute-start.14
  238.7 5.1 collective-permute-done.15
  245.0 3.5 all_to_all.62
  248.5 17.8 %all_to_all.63 = f32[64,2,1,1,128]{4,1,3,2,0:T(2,128)S(1)} all-to-all(f32[64,2,1,1,128]{4,1,3,2,0:T(2,128)S(1)} %copy.75), channel_id=1, replica_groups=mesh['rep'=2,'gx_0'=4,'gx_1'=16,'gx_2'=2] {'gx_0','gx_1'}, dimensions={0} | all-to-all | bytes 131072 | tf_op jit(solution)/shard_map/all_to_all | solution.py:55
  267.5 5.5 all_to_all.64
  273.6 6.5 %all-to-all-start.7 = ((f32[64,2,1,1,128]{4,1,3,2,0:T(2,128)}), f32[64,2,1,1,128]{4,1,3,2,0:T(2,128)S(1)}, u32[]{:S(2)}, u32[]{:S(2)}) async-start(f32[64,2,1,1,128]{4,1,3,2,0:T(2,128)} %copy.77), calls=%async_computation.7 | async-start | bytes 131072 | tf_op jit(solution)/shard_map/all_to_all | solution.py:55
  281.7 2.6 collective-permute-done.21
  284.3 7.9 %all-to-all-done.7 = f32[64,2,1,1,128]{4,1,3,2,0:T(2,128)S(1)} async-done(((f32[64,2,1,1,128]{4,1,3,2,0:T(2,128)}), f32[64,2,1,1,128]{4,1,3,2,0:T(2,128)S(1)}, u32[]{:S(2)}, u32[]{:S(2)}) %all-to-all-start.7) | async-done | bytes 65568 | tf_op jit(solution)/shard_map/all_to_all | solution.py:55
  294.4 48.8 %while.59 = (s32[]{:T(128)}, f32[8,3,128]{2,1,0:T(4,128)S(1)}, s32[8]{0:T(128)S(1)}, s32[8,7]{1,0:T(8,128)}, s32[8]{0:T(128)}, /*index=5*/f32[8,3,128]{2,1,0:T(4...) while((s32[]{:T(128)}, f32[8,3,128]{2,1,0:T(4,128)S(1)}, ...), condition=%wide.region_29.31_spmd.clone, body=%wide.region_25.30_spmd.clone.sunk | while | flops 4610363 | bytes 3891339 | solution.py:102
  343.2 3.0 collective-permute-start.17
  346.2 4.3 collective-permute-start.19
  351.9 5.1 fusion.43
  357.0 3.3 fusion.42
  360.3 1.4 multiply_reduce_fusion.2
  361.7 6.8 %all-reduce.4 = (f32[]{:T(128)}, f32[]{:T(128)}) all-reduce(f32[]{:T(128)} %get-tuple-element.560, f32[]{:T(128)} %get-tuple-element.559), channel_id=1, replica_groups=mesh['rep'=2,'gx_0'=4,'gx_1'=16,'gx_2'=2] {'gx_0'}, use_global_device_ids=true, to_apply=%region_19.21 | all-reduce | flops 2 | bytes 16 | tf_op jit(solution)/shard_map/psum | solution.py:67
  368.5 26.8 %all-reduce.1 = (f32[]{:T(128)}, f32[]{:T(128)}) all-reduce(f32[]{:T(128)} %get-tuple-element.619, f32[]{:T(128)} %get-tuple-element.620), channel_id=1, replica_groups=mesh['rep'=2,'gx_0'=4,'gx_1'=16,'gx_2'=2] {'gx_1'}, use_global_device_ids=true, to_apply=%region_20.22 | all-reduce | flops 2 | bytes 16 | tf_op jit(solution)/shard_map/psum | solution.py:67
  395.3 14.3 %all-reduce.7 = (f32[]{:T(128)}, f32[]{:T(128)}) all-reduce(f32[]{:T(128)} %get-tuple-element.613, f32[]{:T(128)} %get-tuple-element.614), channel_id=1, replica_groups=mesh['rep'=2,'gx_0'=4,'gx_1'=16,'gx_2'=2] {'gx_2'}, use_global_device_ids=true, to_apply=%region_21.23 | all-reduce | flops 2 | bytes 16 | tf_op jit(solution)/shard_map/psum | solution.py:67
  414.4 1.9 broadcast_multiply_fusion
  416.3 2.2 fusion.56
  418.6 2.2 convolution_add_fusion
  421.3 1.4 collective-permute-start.23
  422.7 3.4 collective-permute-start.24
  427.4 5.1 collective-permute-done.25
  433.7 3.5 all_to_all.65
  437.2 18.2 %all_to_all.66 = f32[64,2,1,1,128]{4,1,3,2,0:T(2,128)S(1)} all-to-all(f32[64,2,1,1,128]{4,1,3,2,0:T(2,128)S(1)} %copy.81), channel_id=1, replica_groups=mesh['rep'=2,'gx_0'=4,'gx_1'=16,'gx_2'=2] {'gx_0','gx_1'}, dimensions={0} | all-to-all | bytes 131072 | tf_op jit(solution)/shard_map/all_to_all | solution.py:55
  456.5 5.3 all_to_all.67
  462.5 6.4 %all-to-all-start.11 = ((f32[64,2,1,1,128]{4,1,3,2,0:T(2,128)}), f32[64,2,1,1,128]{4,1,3,2,0:T(2,128)S(1)}, u32[]{:S(2)}, u32[]{:S(2)}) async-start(f32[64,2,1,1,128]{4,1,3,2,0:T(2,128)} %copy.83), calls=%async_computation.11 | async-start | bytes 131072 | tf_op jit(solution)/shard_map/all_to_all | solution.py:55
  470.7 2.6 collective-permute-done.31
  473.3 7.8 %all-to-all-done.11 = f32[64,2,1,1,128]{4,1,3,2,0:T(2,128)S(1)} async-done(((f32[64,2,1,1,128]{4,1,3,2,0:T(2,128)}), f32[64,2,1,1,128]{4,1,3,2,0:T(2,128)S(1)}, u32[]{:S(2)}, u32[]{:S(2)}) %all-to-all-start.11) | async-done | bytes 65568 | tf_op jit(solution)/shard_map/all_to_all | solution.py:55
  482.8 43.5 %while.60 = (s32[]{:T(128)}, f32[8,3,128]{2,1,0:T(4,128)S(1)}, s32[8]{0:T(128)S(1)}, s32[8,7]{1,0:T(8,128)}, s32[8]{0:T(128)S(1)}, /*index=5*/f32[8,3,128]{2,1,0...) while((s32[]{:T(128)}, f32[8,3,128]{2,1,0:T(4,128)S(1)}, ...), condition=%wide.region_45.47_spmd.clone, body=%wide.region_41.46_spmd.clone.sunk | while | flops 4610363 | bytes 3891027 | solution.py:102
  526.4 2.7 collective-permute-start.27
  529.1 4.6 collective-permute-start.29
  533.8 1.5 collective-permute-done.29
  535.3 5.1 fusion.40
  540.4 3.3 fusion.39
  544.4 6.7 %all-reduce.3 = (f32[]{:T(128)}, f32[]{:T(128)}) all-reduce(f32[]{:T(128)} %get-tuple-element.558, f32[]{:T(128)} %get-tuple-element.557), channel_id=1, replica_groups=mesh['rep'=2,'gx_0'=4,'gx_1'=16,'gx_2'=2] {'gx_0'}, use_global_device_ids=true, to_apply=%region_35.37 | all-reduce | flops 2 | bytes 16 | tf_op jit(solution)/shard_map/psum | solution.py:67
  551.1 26.6 %all-reduce = (f32[]{:T(128)}, f32[]{:T(128)}) all-reduce(f32[]{:T(128)} %get-tuple-element.617, f32[]{:T(128)} %get-tuple-element.618), channel_id=1, replica_groups=mesh['rep'=2,'gx_0'=4,'gx_1'=16,'gx_2'=2] {'gx_1'}, use_global_device_ids=true, to_apply=%region_36.38 | all-reduce | flops 2 | bytes 16 | tf_op jit(solution)/shard_map/psum | solution.py:67
  577.7 13.9 %all-reduce.6 = (f32[]{:T(128)}, f32[]{:T(128)}) all-reduce(f32[]{:T(128)} %get-tuple-element.611, f32[]{:T(128)} %get-tuple-element.612), channel_id=1, replica_groups=mesh['rep'=2,'gx_0'=4,'gx_1'=16,'gx_2'=2] {'gx_2'}, use_global_device_ids=true, to_apply=%region_37.39 | all-reduce | flops 2 | bytes 16 | tf_op jit(solution)/shard_map/psum | solution.py:67
  (581 shorter events, 160.2 us)
Async XLA Ops:
  5.5 5.3 copy-start.1
  13.0 33.5 %copy-start.5 = (f32[3,1024]{1,0:T(4,128)S(1)}, f32[3,1024]{1,0:T(4,128)}, u32[]{:S(2)}) copy-start(f32[3,1024]{1,0:T(4,128)} %param.65) | copy-start | bytes 36868
  15.9 34.8 %collective-permute-start = (f32[1,128,128]{2,1,0:T(8,128)}, f32[1,128,128]{2,1,0:T(8,128)}, u32[]{:S(2)}, u32[]{:S(2)}) collective-permute-start(f32[1,128,128]{2,1,0:T(8,128)} %get-tuple-element.678), channel_id=1, source_target_pairs={{0,127},{1,0},{2,1},{3,2},{4,3},{5,4},{6,5},{7,6},{8,7},{9,8},{10,... | collective-permute-start | bytes 196616 | tf_op jit(solution)/shard_map/ppermute | solution.py:24
  36.4 14.9 %collective-permute-start.1 = (f32[1,128,128]{2,1,0:T(8,128)}, f32[1,128,128]{2,1,0:T(8,128)}, u32[]{:S(2)}, u32[]{:S(2)}) collective-permute-start(f32[1,128,128]{2,1,0:T(8,128)} %get-tuple-element.681), channel_id=1, source_target_pairs={{0,1},{1,2},{2,3},{3,4},{4,5},{5,6},{6,7},{7,8},{8,9},{9,10},{10,1... | collective-permute-start | bytes 196616 | tf_op jit(solution)/shard_map/ppermute | solution.py:24
  36.4 16.1 %collective-permute-start.2 = (f32[1,128,128]{2,1,0:T(8,128)}, f32[1,128,128]{2,1,0:T(8,128)}, u32[]{:S(2)}, u32[]{:S(2)}) collective-permute-start(f32[1,128,128]{2,1,0:T(8,128)} %get-tuple-element.680), channel_id=1, source_target_pairs={{0,126},{1,127},{2,0},{3,1},{4,2},{5,3},{6,4},{7,5},{8,6},{9,7},{1... | collective-permute-start | bytes 196616 | tf_op jit(solution)/shard_map/ppermute | solution.py:24
  46.5 9.7 %collective-permute-start.3 = (f32[1,128,128]{2,1,0:T(8,128)}, f32[1,128,128]{2,1,0:T(8,128)}, u32[]{:S(2)}, u32[]{:S(2)}) collective-permute-start(f32[1,128,128]{2,1,0:T(8,128)} %get-tuple-element.679), channel_id=1, source_target_pairs={{0,2},{1,3},{2,4},{3,5},{4,6},{5,7},{6,8},{7,9},{8,10},{9,11},{10,... | collective-permute-start | bytes 196616 | tf_op jit(solution)/shard_map/ppermute | solution.py:24
  47.1 27.6 %collective-permute-start.8 = (f32[3,384]{1,0:T(4,128)}, f32[3,384]{1,0:T(4,128)}, u32[]{:S(2)}, u32[]{:S(2)}) collective-permute-start(f32[3,384]{1,0:T(4,128)} %get-tuple-element.708), channel_id=1, source_target_pairs={{0,1},{1,2},{2,3},{3,4},{4,5},{5,6},{6,7},{7,8},{8,9},{9,10},{10,1... | collective-permute-start | bytes 13832 | tf_op jit(solution)/shard_map/ppermute | solution.py:34
  50.7 24.7 %collective-permute-start.9 = (f32[3,384]{1,0:T(4,128)}, f32[3,384]{1,0:T(4,128)}, u32[]{:S(2)}, u32[]{:S(2)}) collective-permute-start(f32[3,384]{1,0:T(4,128)} %get-tuple-element.707), channel_id=1, source_target_pairs={{1,0},{2,1},{3,2},{4,3},{5,4},{6,5},{7,6},{8,7},{9,8},{10,9},{11,1... | collective-permute-start | bytes 13832 | tf_op jit(solution)/shard_map/ppermute | solution.py:35
  51.2 51.6 %collective-permute-start.10 = (f32[3,384]{1,0:T(4,128)}, f32[3,384]{1,0:T(4,128)}, u32[]{:S(2)}, u32[]{:S(2)}) collective-permute-start(f32[3,384]{1,0:T(4,128)} %get-tuple-element.705), channel_id=1, source_target_pairs={{0,1},{1,2},{2,3},{3,4},{4,5},{5,6},{6,7},{7,8},{8,9},{9,10},{10,1... | collective-permute-start | bytes 13832 | tf_op jit(solution)/shard_map/ppermute | solution.py:34
  52.5 50.3 %collective-permute-start.11 = (f32[3,384]{1,0:T(4,128)}, f32[3,384]{1,0:T(4,128)}, u32[]{:S(2)}, u32[]{:S(2)}) collective-permute-start(f32[3,384]{1,0:T(4,128)} %get-tuple-element.706), channel_id=1, source_target_pairs={{1,0},{2,1},{3,2},{4,3},{5,4},{6,5},{7,6},{8,7},{9,8},{10,9},{11,1... | collective-permute-start | bytes 13832 | tf_op jit(solution)/shard_map/ppermute | solution.py:35
  57.8 45.1 %copy-start.7 = (f32[3,1024]{1,0:T(4,128)S(1)}, f32[3,1024]{1,0:T(4,128)}, u32[]{:S(2)}) copy-start(f32[3,1024]{1,0:T(4,128)} %copy-done.6) | copy-start | bytes 36868
  57.8 56.4 %copy-start.22 = (s32[128]{0:T(128)S(1)}, s32[128]{0:T(128)}, u32[]{:S(2)}) copy-start(s32[128]{0:T(128)} %add_select_fusion.3) | copy-start | bytes 1540
  57.8 56.4 %copy-start.25 = (pred[128]{0:T(512)(128)(4,1)S(1)}, pred[128]{0:T(512)(128)(4,1)}, u32[]{:S(2)}) copy-start(pred[128]{0:T(512)(128)(4,1)} %iota_compare_fusion.7) | copy-start | bytes 388
  57.8 58.0 %copy-start.10 = (s32[8]{0:T(128)S(1)}, s32[8]{0:T(128)}, u32[]{:S(2)}) copy-start(s32[8]{0:T(128)} %param.71) | copy-start | bytes 100
  68.2 18.6 %all-to-all-start.1 = ((f32[64,2,1,1,128]{4,1,3,2,0:T(2,128)}), f32[64,2,1,1,128]{4,1,3,2,0:T(2,128)S(1)}, u32[]{:S(2)}, u32[]{:S(2)}) async-start(f32[64,2,1,1,128]{4,1,3,2,0:T(2,128)} %copy.69), calls=%async_computation.1 | async-start | bytes 131072 | tf_op jit(solution)/shard_map/all_to_all | solution.py:55
  95.5 18.6 %all-to-all-start.3 = ((f32[64,2,1,1,128]{4,1,3,2,0:T(2,128)}), f32[64,2,1,1,128]{4,1,3,2,0:T(2,128)S(1)}, u32[]{:S(2)}, u32[]{:S(2)}) async-start(f32[64,2,1,1,128]{4,1,3,2,0:T(2,128)} %copy.71), calls=%async_computation.3 | async-start | bytes 131072 | tf_op jit(solution)/shard_map/all_to_all | solution.py:55
  115.3 51.7 %collective-permute-start.4 = (f32[1,128,128]{2,1,0:T(8,128)S(1)}, f32[1,128,128]{2,1,0:T(8,128)S(1)}, u32[]{:S(2)}, u32[]{:S(2)}) collective-permute-start(f32[1,128,128]{2,1,0:T(8,128)S(1)} %convolution_bitcast_fusion.2), channel_id=1, source_target_pairs={{0,2},{1,3},{2,4},{3,5},{4,6},{5,7},{6,8},{7,9},{8,10},{9,11},{10,... | collective-permute-start | bytes 196616 | tf_op jit(solution)/shard_map/ppermute | solution.py:24
  159.5 12.6 %copy-start = (f32[1024,5,128]{0,2,1:T(8,128)S(1)}, f32[1024,5,128]{0,2,1:T(8,128)}, u32[]{:S(2)}) copy-start(f32[1024,5,128]{0,2,1:T(8,128)} %get-tuple-element.665) | copy-start | bytes 7864324
  159.5 7.5 %collective-permute-start.5 = (f32[1,128,128]{2,1,0:T(8,128)S(1)}, f32[1,128,128]{2,1,0:T(8,128)S(1)}, u32[]{:S(2)}, u32[]{:S(2)}) collective-permute-start(f32[1,128,128]{2,1,0:T(8,128)S(1)} %convolution_bitcast_fusion.2), channel_id=1, source_target_pairs={{0,1},{1,2},{2,3},{3,4},{4,5},{5,6},{6,7},{7,8},{8,9},{9,10},{10,1... | collective-permute-start | bytes 196616 | tf_op jit(solution)/shard_map/ppermute | solution.py:24
  162.3 4.8 collective-permute-start.6
  162.3 6.4 %collective-permute-start.7 = (f32[1,128,128]{2,1,0:T(8,128)S(1)}, f32[1,128,128]{2,1,0:T(8,128)S(1)}, u32[]{:S(2)}, u32[]{:S(2)}) collective-permute-start(f32[1,128,128]{2,1,0:T(8,128)S(1)} %convolution_bitcast_fusion.2), channel_id=1, source_target_pairs={{0,126},{1,127},{2,0},{3,1},{4,2},{5,3},{6,4},{7,5},{8,6},{9,7},{1... | collective-permute-start | bytes 196616 | tf_op jit(solution)/shard_map/ppermute | solution.py:24
  172.1 4.4 copy-start.4
  172.1 4.4 copy-start.8
  229.6 14.2 %copy-start.23 = (s32[128]{0:T(128)S(1)}, s32[128]{0:T(128)}, u32[]{:S(2)}) copy-start(s32[128]{0:T(128)} %add_select_fusion.3) | copy-start | bytes 1540
  229.7 14.2 %copy-start.26 = (pred[128]{0:T(512)(128)(4,1)S(1)}, pred[128]{0:T(512)(128)(4,1)}, u32[]{:S(2)}) copy-start(pred[128]{0:T(512)(128)(4,1)} %iota_compare_fusion.7) | copy-start | bytes 388
  229.7 36.7 %copy-start.16 = (f32[128]{0:T(128)S(1)}, f32[128]{0:T(128)}, u32[]{:S(2)}) copy-start(f32[128]{0:T(128)} %get-tuple-element.711) | copy-start | bytes 1540
  229.7 36.7 %copy-start.18 = (f32[128]{0:T(128)S(1)}, f32[128]{0:T(128)}, u32[]{:S(2)}) copy-start(f32[128]{0:T(128)} %get-tuple-element.712) | copy-start | bytes 1540
  229.7 36.7 %copy-start.20 = (f32[128]{0:T(128)S(1)}, f32[128]{0:T(128)}, u32[]{:S(2)}) copy-start(f32[128]{0:T(128)} %broadcast_add_fusion) | copy-start | bytes 1540
  231.9 62.5 %copy-start.11 = (s32[8]{0:T(128)S(1)}, s32[8]{0:T(128)}, u32[]{:S(2)}) copy-start(s32[8]{0:T(128)} %param.71) | copy-start | bytes 100
  232.0 5.4 collective-permute-start.12
  232.4 5.0 collective-permute-start.13
  234.0 4.7 collective-permute-start.14
  237.4 6.4 %collective-permute-start.15 = (f32[1,128,128]{2,1,0:T(8,128)S(1)}, f32[1,128,128]{2,1,0:T(8,128)S(1)}, u32[]{:S(2)}, u32[]{:S(2)}) collective-permute-start(f32[1,128,128]{2,1,0:T(8,128)S(1)} %get-tuple-element.675), channel_id=1, source_target_pairs={{0,2},{1,3},{2,4},{3,5},{4,6},{5,7},{6,8},{7,9},{8,10},{9,11},{10,... | collective-permute-start | bytes 196616 | tf_op jit(solution)/shard_map/ppermute | solution.py:24
  273.6 18.6 %all-to-all-start.7 = ((f32[64,2,1,1,128]{4,1,3,2,0:T(2,128)}), f32[64,2,1,1,128]{4,1,3,2,0:T(2,128)S(1)}, u32[]{:S(2)}, u32[]{:S(2)}) async-start(f32[64,2,1,1,128]{4,1,3,2,0:T(2,128)} %copy.77), calls=%async_computation.7 | async-start | bytes 131072 | tf_op jit(solution)/shard_map/all_to_all | solution.py:55
  280.1 1.6 collective-permute-start.20
  280.9 3.4 collective-permute-start.21
  293.4 57.1 %collective-permute-start.16 = (f32[1,128,128]{2,1,0:T(8,128)S(1)}, f32[1,128,128]{2,1,0:T(8,128)S(1)}, u32[]{:S(2)}, u32[]{:S(2)}) collective-permute-start(f32[1,128,128]{2,1,0:T(8,128)S(1)} %convolution_bitcast_fusion.1), channel_id=1, source_target_pairs={{0,2},{1,3},{2,4},{3,5},{4,6},{5,7},{6,8},{7,9},{8,10},{9,11},{10,... | collective-permute-start | bytes 196616 | tf_op jit(solution)/shard_map/ppermute | solution.py:24
  300.5 3.8 copy-start.12
  306.6 3.8 copy-start.12
  312.7 3.8 copy-start.12
  318.8 3.8 copy-start.12
  324.9 3.8 copy-start.12
  343.2 8.7 %copy-start.14 = (s32[8]{0:T(128)}, s32[8]{0:T(128)S(1)}, u32[]{:S(2)}) copy-start(s32[8]{0:T(128)S(1)} %get-tuple-element.1072) | copy-start | bytes 100
  343.2 13.8 %copy-start.9 = (f32[8,3,128]{2,1,0:T(4,128)}, f32[8,3,128]{2,1,0:T(4,128)S(1)}, u32[]{:S(2)}) copy-start(f32[8,3,128]{2,1,0:T(4,128)S(1)} %get-tuple-element.412) | copy-start | bytes 36868
  343.2 7.3 %collective-permute-start.17 = (f32[1,128,128]{2,1,0:T(8,128)S(1)}, f32[1,128,128]{2,1,0:T(8,128)S(1)}, u32[]{:S(2)}, u32[]{:S(2)}) collective-permute-start(f32[1,128,128]{2,1,0:T(8,128)S(1)} %convolution_bitcast_fusion.1), channel_id=1, source_target_pairs={{0,1},{1,2},{2,3},{3,4},{4,5},{5,6},{6,7},{7,8},{8,9},{9,10},{10,1... | collective-permute-start | bytes 196616 | tf_op jit(solution)/shard_map/ppermute | solution.py:24
  346.2 4.4 collective-permute-start.18
  346.2 5.7 collective-permute-start.19
  418.5 14.0 %copy-start.24 = (s32[128]{0:T(128)S(1)}, s32[128]{0:T(128)}, u32[]{:S(2)}) copy-start(s32[128]{0:T(128)} %add_select_fusion.3) | copy-start | bytes 1540
  418.5 14.0 %copy-start.27 = (pred[128]{0:T(512)(128)(4,1)S(1)}, pred[128]{0:T(512)(128)(4,1)}, u32[]{:S(2)}) copy-start(pred[128]{0:T(512)(128)(4,1)} %iota_compare_fusion.7) | copy-start | bytes 388
  418.5 36.8 %copy-start.17 = (f32[128]{0:T(128)S(1)}, f32[128]{0:T(128)}, u32[]{:S(2)}) copy-start(f32[128]{0:T(128)} %get-tuple-element.711) | copy-start | bytes 1540
  418.5 36.8 %copy-start.19 = (f32[128]{0:T(128)S(1)}, f32[128]{0:T(128)}, u32[]{:S(2)}) copy-start(f32[128]{0:T(128)} %get-tuple-element.712) | copy-start | bytes 1540
  418.5 36.8 %copy-start.21 = (f32[128]{0:T(128)S(1)}, f32[128]{0:T(128)}, u32[]{:S(2)}) copy-start(f32[128]{0:T(128)} %broadcast_add_fusion) | copy-start | bytes 1540
  420.8 62.1 %copy-start.15 = (s32[8]{0:T(128)S(1)}, s32[8]{0:T(128)}, u32[]{:S(2)}) copy-start(s32[8]{0:T(128)} %copy-done.14) | copy-start | bytes 100
  420.8 5.3 collective-permute-start.22
  421.3 4.8 collective-permute-start.23
  422.7 4.7 collective-permute-start.24
  426.1 6.4 %collective-permute-start.25 = (f32[1,128,128]{2,1,0:T(8,128)S(1)}, f32[1,128,128]{2,1,0:T(8,128)S(1)}, u32[]{:S(2)}, u32[]{:S(2)}) collective-permute-start(f32[1,128,128]{2,1,0:T(8,128)S(1)} %get-tuple-element.671), channel_id=1, source_target_pairs={{0,2},{1,3},{2,4},{3,5},{4,6},{5,7},{6,8},{7,9},{8,10},{9,11},{10,... | collective-permute-start | bytes 196616 | tf_op jit(solution)/shard_map/ppermute | solution.py:24
  462.5 18.6 %all-to-all-start.11 = ((f32[64,2,1,1,128]{4,1,3,2,0:T(2,128)}), f32[64,2,1,1,128]{4,1,3,2,0:T(2,128)S(1)}, u32[]{:S(2)}, u32[]{:S(2)}) async-start(f32[64,2,1,1,128]{4,1,3,2,0:T(2,128)} %copy.83), calls=%async_computation.11 | async-start | bytes 131072 | tf_op jit(solution)/shard_map/all_to_all | solution.py:55
  469.0 1.7 collective-permute-start.30
  469.9 3.4 collective-permute-start.31
  482.3 51.4 %collective-permute-start.26 = (f32[1,128,128]{2,1,0:T(8,128)S(1)}, f32[1,128,128]{2,1,0:T(8,128)S(1)}, u32[]{:S(2)}, u32[]{:S(2)}) collective-permute-start(f32[1,128,128]{2,1,0:T(8,128)S(1)} %convolution_bitcast_fusion), channel_id=1, source_target_pairs={{0,2},{1,3},{2,4},{3,5},{4,6},{5,7},{6,8},{7,9},{8,10},{9,11},{10,... | collective-permute-start | bytes 196616 | tf_op jit(solution)/shard_map/ppermute | solution.py:24
  526.4 7.3 %collective-permute-start.27 = (f32[1,128,128]{2,1,0:T(8,128)S(1)}, f32[1,128,128]{2,1,0:T(8,128)S(1)}, u32[]{:S(2)}, u32[]{:S(2)}) collective-permute-start(f32[1,128,128]{2,1,0:T(8,128)S(1)} %convolution_bitcast_fusion), channel_id=1, source_target_pairs={{0,1},{1,2},{2,3},{3,4},{4,5},{5,6},{6,7},{7,8},{8,9},{9,10},{10,1... | collective-permute-start | bytes 196616 | tf_op jit(solution)/shard_map/ppermute | solution.py:24
  529.1 4.7 collective-permute-start.28
  529.1 6.1 %collective-permute-start.29 = (f32[1,128,128]{2,1,0:T(8,128)S(1)}, f32[1,128,128]{2,1,0:T(8,128)S(1)}, u32[]{:S(2)}, u32[]{:S(2)}) collective-permute-start(f32[1,128,128]{2,1,0:T(8,128)S(1)} %convolution_bitcast_fusion), channel_id=1, source_target_pairs={{0,126},{1,127},{2,0},{3,1},{4,2},{5,3},{6,4},{7,5},{8,6},{9,7},{1... | collective-permute-start | bytes 196616 | tf_op jit(solution)/shard_map/ppermute | solution.py:24
  (14 other events, 24.9 us)
where the time goes:
time: 608 us; the launch traced here: 596 us
  blocking collectives  210 us (35%)
  starting transfers between devices  98.1 us (16%)
  other arithmetic  74.3 us (12%)
  local copies, waits for them, and re-layouts  73.3 us (12%)
  waiting for transfers between devices  61.2 us (10%)
  matrix products  50.9 us (8%)
  loops' own time  17.2 us (3%)
  between operations  11.6 us (2%)
    psum x9, blocking collectives, over_axes(): x = lax.psum(x, axis)  142 us
    all_to_all x8, blocking collectives, turned_blocks(): lax.all_to_all(tiles, axes[k], split_axis=k, concat_axis=k, tiled=True)  67.6 us
    ppermute x24, starting transfers between devices, from_behind(): lax.ppermute(x, axis, [(i, (i + by) % devices) for i in range(devices)])  65 us
    all_to_all x4, waiting for transfers between devices, turned_blocks(): lax.all_to_all(tiles, axes[k], split_axis=k, concat_axis=k, tiled=True)  37.1 us
    dynamic_slice x48, local copies, waits for them, and re-layouts, pair_field(): lax.scan(one_block, jnp.zeros((), jnp.float32), (home_blocks, tile_rows,...  33.4 us
    and x24, other arithmetic, one_block(): near_pos = jnp.take(pos_blocks, tile_row, axis=1)  31.9 us
    all_to_all x4, starting transfers between devices, turned_blocks(): lax.all_to_all(tiles, axes[k], split_axis=k, concat_axis=k, tiled=True)  25.8 us
    ppermute x24, waiting for transfers between devices, from_behind(): lax.ppermute(x, axis, [(i, (i + by) % devices) for i in range(devices)])  17.3 us
  transfers between devices with their start and end apart: 36, of which 15 were waited for; matrix products, arithmetic and copies ran while one was open for 22% of the time, Pallas kernels for 0%

commit v1 on v0

v1 whole, which is shorter than its diff:
```python
import functools

import jax
import jax.numpy as jnp
import numpy as np
from jax import lax
from jax.experimental import pallas as pl
from jax.experimental.pallas import tpu as pltpu
from jax.sharding import PartitionSpec as P

GRID = 128
ORDER = 5
TILE = 128
HALO_BLK = 3
ITERS = 3
PAIR_C = 0.025
RECIP_C = 8192.0
DAMP = 0.0008
EXACT = lax.Precision.HIGHEST
MESH = pl.DeviceIdType.MESH
F32 = jnp.float32
BF16 = jnp.bfloat16
NX = 4
NC = 2
OFFSETS = (-2, 2, -1, 1)


def far_first(count):
    return sorted(range(1, count), key=lambda d: -min(d, count - d))


def basis(size):
    freq = np.arange(size)
    half = size // 2
    mode = np.where(freq <= half, freq, freq - half)
    angle = (mode[:, None] * np.arange(size)[None, :] % size) * (2.0 * np.pi / size)
    return np.where((freq <= half)[:, None], np.cos(angle), np.sin(angle))


def split(x):
    hi = x.astype(BF16)
    return hi, (x - hi.astype(F32)).astype(BF16)


def exact_dot(a, b):
    return jnp.dot(a, b, precision=EXACT, preferred_element_type=F32)


def fast_dot(a, b):
    return jnp.dot(a, b, preferred_element_type=F32)


def mode_of(freq, size):
    half = size // 2
    mode = jnp.where(freq <= half, freq, freq - half)
    weight = jnp.where((freq == 0) | (freq == half), 1.0 / size, 2.0 / size)
    return mode.astype(F32), weight.astype(F32)


def solve_kernel(
    n,
    tile_list,
    tile_count,
    pos,
    field,
    inv_polar,
    x_spline,
    yz,
    four,
    four_t,
    four_x,
    four_xt,
    dip_out,
    res_out,
    link,
    ext,
    home,
    pair_acc,
    near,
    far,
    y_t,
    dy_t,
    zz,
    zt3,
    lhs_hi,
    lhs_lo,
    rim,
    rim_in,
    pot,
    pot_in,
    pot3,
    green,
    f1_src,
    f1_dst,
    f2_src,
    f2_dst,
    a_src,
    a_dst,
    b_src,
    b_dst,
    ra_src,
    ra_dst,
    rb_src,
    rb_dst,
    vecs,
    scal,
    v_ss,
    v_rs,
    c_ss,
    c_rs,
    h_ss,
    h_rs,
    f1_ss,
    f1_rs,
    f2_ss,
    f2_rs,
    a_ss,
    a_rs,
    b_ss,
    b_rs,
    ra_ss,
    ra_rs,
    rb_ss,
    rb_rs,
):
    nq = NX * NC
    nz = n // nq
    me = lax.axis_index("gx")
    my_q = (me // (nz * NC)) * NC + me % NC
    my_z = me % (nz * NC) // NC
    blocks = pos.shape[1] // TILE
    atoms = pos.shape[1]

    def at(q, z):
        return (q // NC) * (nz * NC) + z * NC + q % NC

    def q_peer(d):
        q = (my_q + d) % nq
        return q, at(q, my_z)

    def z_peer(d):
        z = (my_z + d) % nz
        return z, at(my_q, z)

    def to(d):
        return (me + d + n) % n

    def copy(src, dst, ss, rs, peer):
        return pltpu.make_async_remote_copy(
            src_ref=src, dst_ref=dst, send_sem=ss, recv_sem=rs,
            device_id={"gx": peer}, device_id_type=MESH,
        )

    def rows(i, size):
        return pl.ds(pl.multiple_of(i * size, size), size)

    barrier = pltpu.get_barrier_semaphore()
    for d in far_first(nz):
        pl.semaphore_signal(barrier, inc=1, device_id={"gx": z_peer(d)[1]}, device_id_type=MESH)
    for d in far_first(nq):
        pl.semaphore_signal(barrier, inc=1, device_id={"gx": q_peer(d)[1]}, device_id_type=MESH)
    for d in OFFSETS:
        pl.semaphore_signal(barrier, inc=1, device_id={"gx": to(d)}, device_id_type=MESH)

    def link_row(b, carry):
        for e in range(2 * HALO_BLK + 1):
            total = jnp.float32(0.0)
            for k in range(tile_list.shape[1]):
                hit = (tile_list[b, k] == b + e) & (k < tile_count[b])
                total = total + jnp.where(hit, jnp.float32(1.0), jnp.float32(0.0))
            link[b, e] = total
        return carry

    lax.fori_loop(0, blocks, link_row, 0)

    def prepare(b, carry):
        cols = rows(b, TILE)
        y_t[:, cols] = yz[0, cols, :].T
        dy_t[:, cols] = yz[1, cols, :].T
        for part in range(2):
            z_here = yz[2 + part, cols, :]
            hi, lo = split(z_here)
            at_rows = pl.ds(pl.multiple_of(part * atoms + b * TILE, TILE), TILE)
            zz[at_rows, :GRID] = hi
            zz[at_rows, GRID:] = lo
            hi_t, lo_t = split(z_here.T)
            zt3[:GRID, at_rows] = hi_t
            zt3[GRID : 2 * GRID, at_rows] = hi_t
            zt3[2 * GRID :, at_rows] = lo_t
        here = pos[:, cols]
        for c in range(3):
            home[c, cols, :] = jnp.broadcast_to(here[c : c + 1], (TILE, TILE)).T
        ext[HALO_BLK + b, 3:6, :] = here
        return carry

    lax.fori_loop(0, blocks, prepare, 0)

    row_freq = lax.broadcasted_iota(jnp.int32, (GRID, GRID), 0)
    col_freq = lax.broadcasted_iota(jnp.int32, (GRID, GRID), 1)
    kx, wx = mode_of(row_freq, GRID)
    kz, wz = mode_of(col_freq, GRID)
    ky, wy = mode_of(jnp.full((GRID, GRID), my_q * nz + my_z, jnp.int32), GRID)
    mode_sq = kx * kx + ky * ky + kz * kz
    safe_sq = jnp.where(mode_sq > 0, mode_sq, 1.0)
    green[...] = jnp.where(mode_sq > 0, RECIP_C * jnp.exp(-DAMP * safe_sq) / safe_sq, 0.0) * wx * wy * wz

    ip = inv_polar[...]
    R, U, W, PP, S, Q, Z, X, M = range(9)
    vecs[R] = field[...]
    vecs[U] = field[...] / ip
    vecs[M] = vecs[U]
    for name in (W, PP, S, Q, Z, X):
        vecs[name] = jnp.zeros_like(field)
    scal[...] = jnp.ones_like(scal)
    ra_src[...] = jnp.zeros_like(ra_src)
    pl.semaphore_wait(barrier, (nz - 1) + (nq - 1) + len(OFFSETS))

    def reduce_a():
        return [copy(ra_src, ra_dst.at[my_z], ra_ss.at[d], ra_rs.at[d], z_peer(d)[1]) for d in far_first(nz)]

    def reduce_b():
        return [copy(rb_src, rb_dst.at[my_q], rb_ss.at[d], rb_rs.at[d], q_peer(d)[1]) for d in far_first(nq)]

    def reduce_start():
        g = vecs[R] * vecs[U]
        h = vecs[W] * vecs[U]
        for row, value in ((0, g), (1, h)):
            folded = sum(value[:, k * TILE : (k + 1) * TILE] for k in range(atoms // TILE))
            ra_src[row : row + 1, :] = jnp.sum(folded, axis=0, keepdims=True)
        ra_dst[my_z] = ra_src[...]
        for c in reduce_a():
            c.start()

    def reduce_middle():
        for c in reduce_a():
            c.wait_recv()
        rb_src[...] = jnp.sum(ra_dst[...], axis=0)
        rb_dst[my_q] = rb_src[...]
        for c in reduce_b():
            c.start()

    def reduce_end():
        for c in reduce_b():
            c.wait_recv()
        sums = jnp.sum(jnp.sum(rb_dst[...], axis=0), axis=1, keepdims=True)
        for c in reduce_a():
            c.wait_send()
        for c in reduce_b():
            c.wait_send()
        scal[2] = jnp.broadcast_to(sums, (8, TILE))

    def vec_copies():
        return [
            copy(ext.at[pl.ds(HALO_BLK, HALO_BLK)], ext.at[pl.ds(HALO_BLK + blocks, HALO_BLK)], v_ss.at[0], v_rs.at[0], to(-1)),
            copy(ext.at[pl.ds(blocks, HALO_BLK)], ext.at[pl.ds(0, HALO_BLK)], v_ss.at[1], v_rs.at[1], to(1)),
        ]

    def rim_copy(k):
        return copy(rim.at[k], rim_in.at[k], c_ss.at[k], c_rs.at[k], to(OFFSETS[k]))

    def pot_copy(k):
        return copy(pot, pot_in.at[k], h_ss.at[k], h_rs.at[k], to(OFFSETS[k]))

    def f1_copies():
        out = []
        for d in far_first(nq):
            q, peer = q_peer(d)
            out.append(copy(f1_src.at[rows(q, nz)], f1_dst.at[rows(my_q, nz)], f1_ss.at[d], f1_rs.at[d], peer))
        return out

    def f2_copies():
        out = []
        for d in far_first(nz):
            z, peer = z_peer(d)
            out.append(copy(f2_src.at[rows(z, nq)], f2_dst.at[rows(my_z, nq)], f2_ss.at[d], f2_rs.at[d], peer))
        return out

    def a_copies():
        out = []
        for d in far_first(nz):
            z, peer = z_peer(d)
            out.append(copy(a_src.at[rows(z, nq)], a_dst.at[rows(my_z, nq)], a_ss.at[d], a_rs.at[d], peer))
        return out

    def b_copies():
        out = []
        for d in far_first(nq):
            q, peer = q_peer(d)
            out.append(copy(b_src.at[rows(q, nz)], b_dst.at[rows(my_q, nz)], b_ss.at[d], b_rs.at[d], peer))
        return out

    def spread(planes):
        v = vecs[M]
        for slot, p in enumerate(planes):
            value = x_spline[0, p : p + 1, :]
            slope = x_spline[1, p : p + 1, :]
            band = slice(slot * GRID, (slot + 1) * GRID)
            hi, lo = split(y_t[...] * (v[0:1] * slope) + dy_t[...] * (v[1:2] * value))
            lhs_hi[band, :atoms] = hi
            lhs_lo[band, :atoms] = lo
            hi, lo = split(y_t[...] * (v[2:3] * value))
            lhs_hi[band, atoms:] = hi
            lhs_lo[band, atoms:] = lo
        size = len(planes) * GRID
        wide = fast_dot(lhs_hi[:size, :], zz[...])
        return wide[:, :GRID] + wide[:, GRID:] + fast_dot(lhs_lo[:size, :], zz[:, :GRID])

    chunk = 32

    def pair_block(b, carry):
        v_rows, p_rows = [], []
        for e in range(2 * HALO_BLK + 1):
            tile = ext[b + e]
            shift = jnp.where(b + e < HALO_BLK, -1.0 * blocks, jnp.where(b + e >= HALO_BLK + blocks, 1.0 * blocks, 0.0)).astype(F32)
            v_rows.append(tile[0:3] * link[b, e])
            p_rows.append((tile[3:4] + shift, tile[4:5], tile[5:6]))

        def strip(i, inner):
            at_rows = pl.ds(pl.multiple_of(b * TILE + i * chunk, chunk), chunk)
            hx, hy, hz = home[0, at_rows, :], home[1, at_rows, :], home[2, at_rows, :]
            ax = jnp.zeros((chunk, TILE), F32)
            ay, az = ax, ax
            for e in range(2 * HALO_BLK + 1):
                px, py, pz = p_rows[e]
                vx, vy, vz = v_rows[e][0:1], v_rows[e][1:2], v_rows[e][2:3]
                dx, dy, dz = hx - px, hy - py, hz - pz
                inverse = lax.rsqrt(dx * dx + dy * dy + dz * dz + 1.0)
                inverse_sq = inverse * inverse
                third = inverse_sq * inverse
                along = (dx * vx + dy * vy + dz * vz) * (third * inverse_sq) * 3.0
                ax = ax + (third * vx - along * dx)
                ay = ay + (third * vy - along * dy)
                az = az + (third * vz - along * dz)
            pair_acc[0, at_rows, :] = ax
            pair_acc[1, at_rows, :] = ay
            pair_acc[2, at_rows, :] = az
            return inner

        lax.fori_loop(0, TILE // chunk, strip, 0)
        cols = rows(b, TILE)
        for c in range(3):
            near[c : c + 1, cols] = jnp.sum(pair_acc[c, cols, :].T, axis=0, keepdims=True)
        return carry

    def gather_chunk(g, carry):
        wide = 256
        cols = rows(g, wide)
        plain = fast_dot(pot3[...], zt3[:, cols])
        sa = jnp.zeros((GRID, wide), F32)
        sb = sa
        for p in range(ORDER):
            band = plain[p * GRID : (p + 1) * GRID]
            sa = sa + x_spline[1, p : p + 1, cols] * band
            sb = sb + x_spline[0, p : p + 1, cols] * band
        far[0:1, cols] = jnp.sum(sa * y_t[:, cols], axis=0, keepdims=True)
        far[1:2, cols] = jnp.sum(sb * dy_t[:, cols], axis=0, keepdims=True)
        tilted = fast_dot(pot3[...], zt3[:, pl.ds(pl.multiple_of(atoms + g * wide, wide), wide)])
        sc = jnp.zeros((GRID, wide), F32)
        for p in range(ORDER):
            sc = sc + x_spline[0, p : p + 1, cols] * tilted[p * GRID : (p + 1) * GRID]
        far[2:3, cols] = jnp.sum(sc * y_t[:, cols], axis=0, keepdims=True)
        return carry

    def put_plane(p, plane):
        hi, lo = split(plane)
        band = slice(p * GRID, (p + 1) * GRID)
        pot3[band, :GRID] = hi
        pot3[band, GRID : 2 * GRID] = lo
        pot3[band, 2 * GRID :] = hi

    def sweep(it, carry):
        v = vecs[M]
        for b in range(blocks):
            ext[HALO_BLK + b, 0:3, :] = v[:, b * TILE : (b + 1) * TILE]
        for c in vec_copies():
            c.start()
        for pair in ((0, 1), (2, 3)):
            both = spread([OFFSETS[k] + 2 for k in pair])
            for slot, k in enumerate(pair):
                rim[k] = both[slot * GRID : (slot + 1) * GRID]
                rim_copy(k).start()
        own = spread([2])
        for k in range(len(OFFSETS)):
            rim_copy(k).wait_recv()
            own = own + rim_in[k]
        along_z = exact_dot(own, four_t[...])
        f1_src[...] = exact_dot(four[...], along_z)
        for c in f1_copies():
            c.start()
        f1_dst[rows(my_q, nz), :] = f1_src[rows(my_q, nz), :]

        for c in vec_copies():
            c.wait_recv()
        lax.fori_loop(0, 2, pair_block, 0)

        @pl.when(it > 0)
        def _():
            reduce_middle()

        for c in f1_copies():
            c.wait_recv()
        for z in range(nz):
            f2_src[z * nq : (z + 1) * nq, :] = f1_dst[pl.ds(z, nq, stride=nz), :]
        for c in f2_copies():
            c.start()
        f2_dst[rows(my_z, nq), :] = f2_src[rows(my_z, nq), :]

        lax.fori_loop(2, blocks, pair_block, 0)

        @pl.when(it > 0)
        def _():
            reduce_end()

        for c in f2_copies():
            c.wait_recv()
        lines = exact_dot(four_x[...], f2_dst[...]) * green[...]
        a_src[...] = exact_dot(four_xt[...], lines)
        for c in a_copies():
            c.start()
        a_dst[rows(my_z, nq), :] = a_src[rows(my_z, nq), :]
        for c in a_copies():
            c.wait_recv()
        for q in range(nq):
            b_src[q * nz : (q + 1) * nz, :] = a_dst[pl.ds(q, nz, stride=nq), :]
        for c in b_copies():
            c.start()
        b_dst[rows(my_q, nz), :] = b_src[rows(my_q, nz), :]
        for c in b_copies():
            c.wait_recv()
        along_k = exact_dot(four_t[...], b_dst[...])
        mine = exact_dot(along_k, four[...])
        pot[...] = mine
        for k in range(len(OFFSETS)):
            pot_copy(k).start()
        put_plane(2, mine)
        for k in range(len(OFFSETS)):
            pot_copy(k).wait_recv()
            put_plane(2 - OFFSETS[k], pot_in[k])
        lax.fori_loop(0, atoms // 256, gather_chunk, 0)
        image = ip * v + far[...] - PAIR_C * (near[...] - v)

        @pl.when(it == 0)
        def _():
            vecs[W] = image

        @pl.when(it > 0)
        def _():
            gamma = scal[2, 0:1, 0:1]
            delta = scal[2, 1:2, 0:1]
            beta = jnp.where(it == 1, 0.0, gamma / scal[0, 0:1, 0:1])
            alpha = gamma / (delta - beta * gamma / scal[1, 0:1, 0:1])
            scal[0] = jnp.broadcast_to(gamma, (8, TILE))
            scal[1] = jnp.broadcast_to(alpha, (8, TILE))
            new_z = image + beta * vecs[Z]
            new_q = v + beta * vecs[Q]
            new_s = vecs[W] + beta * vecs[S]
            new_p = vecs[U] + beta * vecs[PP]
            vecs[Z] = new_z
            vecs[Q] = new_q
            vecs[S] = new_s
            vecs[PP] = new_p
            vecs[X] = vecs[X] + alpha * new_p
            vecs[R] = vecs[R] - alpha * new_s
            vecs[U] = vecs[U] - alpha * new_q
            vecs[W] = vecs[W] - alpha * new_z

        reduce_start()
        vecs[M] = vecs[W] / ip
        for group in (vec_copies(), f1_copies(), f2_copies(), a_copies(), b_copies()):
            for c in group:
                c.wait_send()
        for k in range(len(OFFSETS)):
            rim_copy(k).wait_send()
            pot_copy(k).wait_send()
        return carry

    lax.fori_loop(0, ITERS, sweep, 0)
    reduce_middle()
    reduce_end()
    gamma = scal[2, 0:1, 0:1]
    delta = scal[2, 1:2, 0:1]
    beta = gamma / scal[0, 0:1, 0:1]
    alpha = gamma / (delta - beta * gamma / scal[1, 0:1, 0:1])
    dip_out[...] = vecs[X] + alpha * (vecs[U] + beta * vecs[PP])
    res_out[...] = vecs[R] - alpha * (vecs[W] + beta * vecs[S])


def per_device(n, positions, field, inv_polar, x_spline, yz_spline, tile_list, tile_count):
    atoms = positions.shape[1]
    blocks = atoms // TILE
    nq = NX * NC
    nz = n // nq
    rows_x = np.arange(GRID)
    q, z = rows_x % nq, rows_x // nq
    plane = (q // NC) * (nz * NC) + z * NC + q % NC
    table = basis(GRID)
    four = jnp.asarray(table, F32)
    four_t = jnp.asarray(table.T.copy(), F32)
    four_x = jnp.asarray(table[:, plane], F32)
    four_xt = jnp.asarray(table[:, plane].T.copy(), F32)
    vm = pl.BlockSpec(memory_space=pltpu.VMEM)
    sm = pl.BlockSpec(memory_space=pltpu.SMEM)
    square = pltpu.VMEM((GRID, GRID), F32)
    sem = pltpu.SemaphoreType.DMA
    out = jax.ShapeDtypeStruct((3, atoms), F32)
    return pl.pallas_call(
        functools.partial(solve_kernel, n),
        out_shape=(out, out),
        in_specs=[sm, sm] + [vm] * 9,
        out_specs=(vm, vm),
        scratch_shapes=[
            pltpu.SMEM((blocks, 2 * HALO_BLK + 1), F32),
            pltpu.VMEM((blocks + 2 * HALO_BLK, 8, TILE), F32),
            pltpu.VMEM((3, atoms, TILE), F32),
            pltpu.VMEM((3, atoms, TILE), F32),
            pltpu.VMEM((3, atoms), F32),
            pltpu.VMEM((3, atoms), F32),
            pltpu.VMEM((GRID, atoms), F32),
            pltpu.VMEM((GRID, atoms), F32),
            pltpu.VMEM((2 * atoms, 2 * GRID), BF16),
            pltpu.VMEM((3 * GRID, 2 * atoms), BF16),
            pltpu.VMEM((2 * GRID, 2 * atoms), BF16),
            pltpu.VMEM((2 * GRID, 2 * atoms), BF16),
            pltpu.VMEM((4, GRID, GRID), F32),
            pltpu.VMEM((4, GRID, GRID), F32),
            square,
            pltpu.VMEM((4, GRID, GRID), F32),
            pltpu.VMEM((ORDER * GRID, 3 * GRID), BF16),
            square,
            square, square, square, square,
            square, square, square, square,
            pltpu.VMEM((8, TILE), F32),
            pltpu.VMEM((nz, 8, TILE), F32),
            pltpu.VMEM((8, TILE), F32),
            pltpu.VMEM((nq, 8, TILE), F32),
            pltpu.VMEM((9, 3, atoms), F32),
            pltpu.VMEM((3, 8, TILE), F32),
            sem((2,)), sem((2,)),
            sem((4,)), sem((4,)),
            sem((4,)), sem((4,)),
            sem((nq,)), sem((nq,)),
            sem((nz,)), sem((nz,)),
            sem((nz,)), sem((nz,)),
            sem((nq,)), sem((nq,)),
            sem((nz,)), sem((nz,)),
            sem((nq,)), sem((nq,)),
        ],
        compiler_params=pltpu.CompilerParams(
            collective_id=0, has_side_effects=True, vmem_limit_bytes=56 * 1024 * 1024
        ),
    )(tile_list, tile_count, positions, field, inv_polar.reshape(1, atoms), x_spline, yz_spline,
      four, four_t, four_x, four_xt)


def solution(mesh):
    both = ("rep", "gx")
    in_specs = (
        P(None, both),
        P(None, both),
        P(both),
        P(None, None, both),
        P(None, both, None),
        P(both, None),
        P(both),
    )
    out_specs = (P(None, both), P(None, both))
    return jax.shard_map(
        functools.partial(per_device, mesh.shape["gx"]),
        mesh=mesh, in_specs=in_specs, out_specs=out_specs, check_vma=False,
    )
```

time: 608 us -> 156 us (0.26); the launches traced: 596 us -> 156 us
  blocking collectives: 210 us -> 0 us
  Pallas kernels: 0 us -> 151 us
  starting transfers between devices: 98.1 us -> 0 us
  other arithmetic: 74.3 us -> 0 us
  local copies, waits for them, and re-layouts: 73.3 us -> 4.07 us
  waiting for transfers between devices: 61.2 us -> 0 us
  matrix products: 50.9 us -> 0 us
  loops' own time: 17.2 us -> 0 us
  between operations: 11.6 us -> 0.64 us
    pallas_call x0 -> x1, Pallas kernels: none -> 151 us  [per_device(): pl.pallas_call(functools.partial(solve_kernel, n), out_shape=(out, out),...]
    psum x9 -> x0, blocking collectives: 142 us -> none  [over_axes(): x = lax.psum(x, axis)]
    ppermute x32 -> x0, starting transfers between devices: 72.2 us -> none  [the longest x24 65 us: from_behind(): lax.ppermute(x, axis, [(i, (i + by) % devices) for i in range(devices)])]
    all_to_all x8 -> x0, blocking collectives: 67.6 us -> none  [turned_blocks(): lax.all_to_all(tiles, axes[k], split_axis=k, concat_axis=k, tiled=True)]
    dot_general x30 -> x0, matrix products: 50.9 us -> none  [the longest x3 14.5 us: gather_field(): lax.dot_general(yz_spline[2], flat_grid, contract, precision=EXACT)]
    all_to_all x4 -> x0, waiting for transfers between devices: 37.1 us -> none  [turned_blocks(): lax.all_to_all(tiles, axes[k], split_axis=k, concat_axis=k, tiled=True)]
    dynamic_slice x48 -> x0, local copies, waits for them, and re-layouts: 33.4 us -> none  [pair_field(): lax.scan(one_block, jnp.zeros((), jnp.float32), (home_blocks, tile_rows,...]
    and x24 -> x0, other arithmetic: 31.9 us -> none  [one_block(): near_pos = jnp.take(pos_blocks, tile_row, axis=1)]
  transfers between devices with their start and end apart: 36 -> 0, of which waited for: 15 -> 0; matrix products, arithmetic and copies ran while one was open for 22% -> 0% of each run, Pallas kernels for 0% -> 0%
where the time goes in v1:
time: 156 us
  Pallas kernels  151 us (97%)
  local copies, waits for them, and re-layouts  4.07 us (3%)
    pallas_call x1, Pallas kernels, per_device(): pl.pallas_call(functools.partial(solve_kernel, n), out_shape=(out, out),...  151 us
    unnamed x3, local copies, waits for them, and re-layouts  4.07 us

profile of v1, /device:TPU:33, one launch (start us, length us, event | category | flops | bytes accessed | tf_op | source)
XLA Modules:
  0.0 155.6 jit_solution(5605679205498208307)
XLA Ops:
  0.6 1.4 copy.13.x_spline
  2.0 150.9 %shard_map.122 = (f32[3,1024]{1,0:T(4,128)}, f32[3,1024]{1,0:T(4,128)}) custom-call(s32[8,7]{1,0:T(8,128)} %tile_list.1, s32[8]{0:T(128)} %tile_count.1, f32[3,1024]{1,0:T(4,128)} %pos.1, f32[3,1024]{1,0:T(4,128)} %field.1, f32[1,1024]{1,0:T(1,128)} %bitcast.1, f32[2,5,1024]{2,1,0:T(8,128)} %copy.13.x_spline, f32[4,1024,128]{2,1,0:T(8,128)} %yz.1, ...), custom_call_target="tpu_custom_call" | custom-call | tf_op jit(solution)/shard_map/pallas_call | solution.py:506
  152.9 1.3 copy.16
  154.3 1.3 copy.17

commit v2 on v1

--- a/solution.py
+++ b/solution.py
@@ -70,8 +70,11 @@
     four_t,
     four_x,
     four_xt,
-    dip_out,
-    res_out,
+    dip_a,
+    dip_b,
+    res_a,
+    res_b,
+    step_out,
     link,
     ext,
     home,
@@ -81,14 +84,15 @@
     y_t,
     dy_t,
     zz,
-    zt3,
+    zt4,
     lhs_hi,
     lhs_lo,
     rim,
     rim_in,
+    own_plane,
     pot,
     pot_in,
-    pot3,
+    pot4,
     green,
     f1_src,
     f1_dst,
@@ -162,7 +166,30 @@
     for d in OFFSETS:
         pl.semaphore_signal(barrier, inc=1, device_id={"gx": to(d)}, device_id_type=MESH)
 
-    def link_row(b, carry):
+    def prepare(b, carry):
+        cols = rows(b, TILE)
+        y_t[:, cols] = yz[0, cols, :].T
+        dy_t[:, cols] = yz[1, cols, :].T
+        for part in range(2):
+            hi, lo = split(yz[2 + part, cols, :])
+            at_rows = pl.ds(pl.multiple_of(part * atoms + b * TILE, TILE), TILE)
+            zz[at_rows, :GRID] = hi
+            zz[at_rows, GRID:] = lo
+        ext[HALO_BLK + b, 3:6, :] = pos[:, cols]
+        return carry
+
+    def prepare_more(b, carry):
+        cols = rows(b, TILE)
+        for part in range(2):
+            at_rows = pl.ds(pl.multiple_of(part * atoms + b * TILE, TILE), TILE)
+            hi, lo = split(yz[2 + part, cols, :].T)
+            zt4[:GRID, at_rows] = hi
+            zt4[GRID : 2 * GRID, at_rows] = hi
+            zt4[2 * GRID : 3 * GRID, at_rows] = lo
+            zt4[3 * GRID :, at_rows] = lo
+        here = pos[:, cols]
+        for c in range(3):
+            home[c, cols, :] = jnp.broadcast_to(here[c : c + 1], (TILE, TILE)).T
         for e in range(2 * HALO_BLK + 1):
             total = jnp.float32(0.0)
             for k in range(tile_list.shape[1]):
@@ -171,49 +198,18 @@
             link[b, e] = total
         return carry
 
-    lax.fori_loop(0, blocks, link_row, 0)
-
-    def prepare(b, carry):
-        cols = rows(b, TILE)
-        y_t[:, cols] = yz[0, cols, :].T
-        dy_t[:, cols] = yz[1, cols, :].T
-        for part in range(2):
-            z_here = yz[2 + part, cols, :]
-            hi, lo = split(z_here)
-            at_rows = pl.ds(pl.multiple_of(part * atoms + b * TILE, TILE), TILE)
-            zz[at_rows, :GRID] = hi
-            zz[at_rows, GRID:] = lo
-            hi_t, lo_t = split(z_here.T)
-            zt3[:GRID, at_rows] = hi_t
-            zt3[GRID : 2 * GRID, at_rows] = hi_t
-            zt3[2 * GRID :, at_rows] = lo_t
-        here = pos[:, cols]
-        for c in range(3):
-            home[c, cols, :] = jnp.broadcast_to(here[c : c + 1], (TILE, TILE)).T
-        ext[HALO_BLK + b, 3:6, :] = here
-        return carry
-
-    lax.fori_loop(0, blocks, prepare, 0)
-
-    row_freq = lax.broadcasted_iota(jnp.int32, (GRID, GRID), 0)
-    col_freq = lax.broadcasted_iota(jnp.int32, (GRID, GRID), 1)
-    kx, wx = mode_of(row_freq, GRID)
-    kz, wz = mode_of(col_freq, GRID)
-    ky, wy = mode_of(jnp.full((GRID, GRID), my_q * nz + my_z, jnp.int32), GRID)
-    mode_sq = kx * kx + ky * ky + kz * kz
-    safe_sq = jnp.where(mode_sq > 0, mode_sq, 1.0)
-    green[...] = jnp.where(mode_sq > 0, RECIP_C * jnp.exp(-DAMP * safe_sq) / safe_sq, 0.0) * wx * wy * wz
+    def prepare_green():
+        row_freq = lax.broadcasted_iota(jnp.int32, (GRID, GRID), 0)
+        col_freq = lax.broadcasted_iota(jnp.int32, (GRID, GRID), 1)
+        kx, wx = mode_of(row_freq, GRID)
+        kz, wz = mode_of(col_freq, GRID)
+        ky, wy = mode_of(jnp.full((GRID, GRID), my_q * nz + my_z, jnp.int32), GRID)
+        mode_sq = kx * kx + ky * ky + kz * kz
+        safe_sq = jnp.where(mode_sq > 0, mode_sq, 1.0)
+        green[...] = jnp.where(mode_sq > 0, RECIP_C * jnp.exp(-DAMP * safe_sq) / safe_sq, 0.0) * wx * wy * wz
 
     ip = inv_polar[...]
-    R, U, W, PP, S, Q, Z, X, M = range(9)
-    vecs[R] = field[...]
-    vecs[U] = field[...] / ip
-    vecs[M] = vecs[U]
-    for name in (W, PP, S, Q, Z, X):
-        vecs[name] = jnp.zeros_like(field)
-    scal[...] = jnp.ones_like(scal)
-    ra_src[...] = jnp.zeros_like(ra_src)
-    pl.semaphore_wait(barrier, (nz - 1) + (nq - 1) + len(OFFSETS))
+    R, U, PP, S, X = range(5)
 
     def reduce_a():
         return [copy(ra_src, ra_dst.at[my_z], ra_ss.at[d], ra_rs.at[d], z_peer(d)[1]) for d in far_first(nz)]
@@ -221,12 +217,14 @@
     def reduce_b():
         return [copy(rb_src, rb_dst.at[my_q], rb_ss.at[d], rb_rs.at[d], q_peer(d)[1]) for d in far_first(nq)]
 
-    def reduce_start():
-        g = vecs[R] * vecs[U]
-        h = vecs[W] * vecs[U]
-        for row, value in ((0, g), (1, h)):
-            folded = sum(value[:, k * TILE : (k + 1) * TILE] for k in range(atoms // TILE))
-            ra_src[row : row + 1, :] = jnp.sum(folded, axis=0, keepdims=True)
+    def folded(value):
+        lanes = sum(value[:, k * TILE : (k + 1) * TILE] for k in range(atoms // TILE))
+        return jnp.sum(lanes, axis=0, keepdims=True)
+
+    def reduce_start(energy):
+        u = vecs[U]
+        ra_src[0:1, :] = folded(vecs[R] * u)
+        ra_src[1:2, :] = folded((ip * u - PAIR_C * (near[...] - u)) * u) + energy
         ra_dst[my_z] = ra_src[...]
         for c in reduce_a():
             c.start()
@@ -247,7 +245,7 @@
             c.wait_send()
         for c in reduce_b():
             c.wait_send()
-        scal[2] = jnp.broadcast_to(sums, (8, TILE))
+        return sums[0:1], sums[1:2]
 
     def vec_copies():
         return [
@@ -290,10 +288,10 @@
         return out
 
     def spread(planes):
-        v = vecs[M]
+        v = vecs[U]
         for slot, p in enumerate(planes):
-            value = x_spline[0, p : p + 1, :]
-            slope = x_spline[1, p : p + 1, :]
+            value = x_spline[p, 0:1, :]
+            slope = x_spline[p, 1:2, :]
             band = slice(slot * GRID, (slot + 1) * GRID)
             hi, lo = split(y_t[...] * (v[0:1] * slope) + dy_t[...] * (v[1:2] * value))
             lhs_hi[band, :atoms] = hi
@@ -302,8 +300,8 @@
             lhs_hi[band, atoms:] = hi
             lhs_lo[band, atoms:] = lo
         size = len(planes) * GRID
-        wide = fast_dot(lhs_hi[:size, :], zz[...])
-        return wide[:, :GRID] + wide[:, GRID:] + fast_dot(lhs_lo[:size, :], zz[:, :GRID])
+        wide = fast_dot(lhs_hi[:size, :], zz[...]) + fast_dot(lhs_lo[:size, :], zz[...])
+        return wide[:, :GRID] + wide[:, GRID:]
 
     chunk = 32
 
@@ -345,41 +343,59 @@
     def gather_chunk(g, carry):
         wide = 256
         cols = rows(g, wide)
-        plain = fast_dot(pot3[...], zt3[:, cols])
+        plain = fast_dot(pot4[...], zt4[:, cols])
         sa = jnp.zeros((GRID, wide), F32)
         sb = sa
         for p in range(ORDER):
             band = plain[p * GRID : (p + 1) * GRID]
-            sa = sa + x_spline[1, p : p + 1, cols] * band
-            sb = sb + x_spline[0, p : p + 1, cols] * band
+            sa = sa + x_spline[p, 1:2, cols] * band
+            sb = sb + x_spline[p, 0:1, cols] * band
         far[0:1, cols] = jnp.sum(sa * y_t[:, cols], axis=0, keepdims=True)
         far[1:2, cols] = jnp.sum(sb * dy_t[:, cols], axis=0, keepdims=True)
-        tilted = fast_dot(pot3[...], zt3[:, pl.ds(pl.multiple_of(atoms + g * wide, wide), wide)])
+        tilted = fast_dot(pot4[...], zt4[:, pl.ds(pl.multiple_of(atoms + g * wide, wide), wide)])
         sc = jnp.zeros((GRID, wide), F32)
         for p in range(ORDER):
-            sc = sc + x_spline[0, p : p + 1, cols] * tilted[p * GRID : (p + 1) * GRID]
+            sc = sc + x_spline[p, 0:1, cols] * tilted[p * GRID : (p + 1) * GRID]
         far[2:3, cols] = jnp.sum(sc * y_t[:, cols], axis=0, keepdims=True)
         return carry
 
     def put_plane(p, plane):
         hi, lo = split(plane)
         band = slice(p * GRID, (p + 1) * GRID)
-        pot3[band, :GRID] = hi
-        pot3[band, GRID : 2 * GRID] = lo
-        pot3[band, 2 * GRID :] = hi
-
-    def sweep(it, carry):
-        v = vecs[M]
+        pot4[band, :GRID] = hi
+        pot4[band, GRID : 2 * GRID] = lo
+        pot4[band, 2 * GRID : 3 * GRID] = hi
+        pot4[band, 3 * GRID :] = lo
+
+    def put_vector():
+        v = vecs[U]
         for b in range(blocks):
             ext[HALO_BLK + b, 0:3, :] = v[:, b * TILE : (b + 1) * TILE]
-        for c in vec_copies():
-            c.start()
-        for pair in ((0, 1), (2, 3)):
-            both = spread([OFFSETS[k] + 2 for k in pair])
-            for slot, k in enumerate(pair):
-                rim[k] = both[slot * GRID : (slot + 1) * GRID]
-                rim_copy(k).start()
-        own = spread([2])
+
+    def spread_pair(pair):
+        both = spread([OFFSETS[k] + 2 for k in pair])
+        for slot, k in enumerate(pair):
+            rim[k] = both[slot * GRID : (slot + 1) * GRID]
+
+    lax.fori_loop(0, blocks, prepare, 0)
+    vecs[R] = field[...]
+    vecs[U] = field[...] / ip
+    for name in (PP, S, X):
+        vecs[name] = jnp.zeros((3, atoms), F32)
+    scal[...] = jnp.ones_like(scal)
+    ra_src[...] = jnp.zeros_like(ra_src)
+    put_vector()
+    spread_pair((0, 1))
+    spread_pair((2, 3))
+    pl.semaphore_wait(barrier, (nz - 1) + (nq - 1) + len(OFFSETS))
+    for k in range(len(OFFSETS)):
+        rim_copy(k).start()
+    for c in vec_copies():
+        c.start()
+    own_plane[...] = spread([2])
+
+    def sweep(it, carry):
+        own = own_plane[...]
         for k in range(len(OFFSETS)):
             rim_copy(k).wait_recv()
             own = own + rim_in[k]
@@ -389,13 +405,14 @@
             c.start()
         f1_dst[rows(my_q, nz), :] = f1_src[rows(my_q, nz), :]
 
+        @pl.when(it == 0)
+        def _():
+            lax.fori_loop(0, blocks, prepare_more, 0)
+            prepare_green()
+
         for c in vec_copies():
             c.wait_recv()
         lax.fori_loop(0, 2, pair_block, 0)
-
-        @pl.when(it > 0)
-        def _():
-            reduce_middle()
 
         for c in f1_copies():
             c.wait_recv()
@@ -407,17 +424,15 @@
 
         lax.fori_loop(2, blocks, pair_block, 0)
 
-        @pl.when(it > 0)
-        def _():
-            reduce_end()
-
         for c in f2_copies():
             c.wait_recv()
-        lines = exact_dot(four_x[...], f2_dst[...]) * green[...]
-        a_src[...] = exact_dot(four_xt[...], lines)
+        lines = exact_dot(four_x[...], f2_dst[...])
+        scaled = lines * green[...]
+        a_src[...] = exact_dot(four_xt[...], scaled)
         for c in a_copies():
             c.start()
         a_dst[rows(my_z, nq), :] = a_src[rows(my_z, nq), :]
+        reduce_start(jnp.sum(lines * scaled, axis=0, keepdims=True))
         for c in a_copies():
             c.wait_recv()
         for q in range(nq):
@@ -425,64 +440,64 @@
         for c in b_copies():
             c.start()
         b_dst[rows(my_q, nz), :] = b_src[rows(my_q, nz), :]
+        reduce_middle()
         for c in b_copies():
             c.wait_recv()
         along_k = exact_dot(four_t[...], b_dst[...])
         mine = exact_dot(along_k, four[...])
         pot[...] = mine
-        for k in range(len(OFFSETS)):
+        for k in (2, 3, 0, 1):
             pot_copy(k).start()
         put_plane(2, mine)
-        for k in range(len(OFFSETS)):
-            pot_copy(k).wait_recv()
-            put_plane(2 - OFFSETS[k], pot_in[k])
-        lax.fori_loop(0, atoms // 256, gather_chunk, 0)
-        image = ip * v + far[...] - PAIR_C * (near[...] - v)
-
-        @pl.when(it == 0)
-        def _():
-            vecs[W] = image
-
-        @pl.when(it > 0)
-        def _():
-            gamma = scal[2, 0:1, 0:1]
-            delta = scal[2, 1:2, 0:1]
-            beta = jnp.where(it == 1, 0.0, gamma / scal[0, 0:1, 0:1])
-            alpha = gamma / (delta - beta * gamma / scal[1, 0:1, 0:1])
-            scal[0] = jnp.broadcast_to(gamma, (8, TILE))
-            scal[1] = jnp.broadcast_to(alpha, (8, TILE))
-            new_z = image + beta * vecs[Z]
-            new_q = v + beta * vecs[Q]
-            new_s = vecs[W] + beta * vecs[S]
-            new_p = vecs[U] + beta * vecs[PP]
-            vecs[Z] = new_z
-            vecs[Q] = new_q
-            vecs[S] = new_s
-            vecs[PP] = new_p
-            vecs[X] = vecs[X] + alpha * new_p
-            vecs[R] = vecs[R] - alpha * new_s
-            vecs[U] = vecs[U] - alpha * new_q
-            vecs[W] = vecs[W] - alpha * new_z
-
-        reduce_start()
-        vecs[M] = vecs[W] / ip
         for group in (vec_copies(), f1_copies(), f2_copies(), a_copies(), b_copies()):
             for c in group:
                 c.wait_send()
         for k in range(len(OFFSETS)):
             rim_copy(k).wait_send()
+        for k in (2, 3, 0, 1):
+            pot_copy(k).wait_recv()
+            put_plane(2 - OFFSETS[k], pot_in[k])
+        lax.fori_loop(0, atoms // 256, gather_chunk, 0)
+        u = vecs[U]
+        image = ip * u + far[...] - PAIR_C * (near[...] - u)
+        gamma, delta = reduce_end()
+        beta = jnp.where(it == 0, 0.0, gamma / scal[0, 0:1, 0:1])
+        alpha = gamma / (delta - beta * gamma / scal[1, 0:1, 0:1])
+        scal[0] = jnp.broadcast_to(gamma, (8, TILE))
+        scal[1] = jnp.broadcast_to(alpha, (8, TILE))
+        new_p = u + beta * vecs[PP]
+        new_s = image + beta * vecs[S]
+        vecs[PP] = new_p
+        vecs[S] = new_s
+
+        @pl.when(it < ITERS - 1)
+        def _():
+            residual = vecs[R] - alpha * new_s
+            vecs[U] = residual / ip
+            put_vector()
+            for c in vec_copies():
+                c.start()
+            vecs[R] = residual
+            vecs[X] = vecs[X] + alpha * new_p
+            for pair in ((0, 1), (2, 3)):
+                spread_pair(pair)
+                for k in pair:
+                    rim_copy(k).start()
+            own_plane[...] = spread([2])
+
+        @pl.when(it == ITERS - 1)
+        def _():
+            dip_a[...] = vecs[X]
+            dip_b[...] = new_p
+            step_out[...] = jnp.broadcast_to(alpha, (3, atoms))
+            res_a[...] = vecs[R]
+            res_b[...] = new_s
+
+        for k in range(len(OFFSETS)):
             pot_copy(k).wait_send()
         return carry
 
     lax.fori_loop(0, ITERS, sweep, 0)
-    reduce_middle()
-    reduce_end()
-    gamma = scal[2, 0:1, 0:1]
-    delta = scal[2, 1:2, 0:1]
-    beta = gamma / scal[0, 0:1, 0:1]
-    alpha = gamma / (delta - beta * gamma / scal[1, 0:1, 0:1])
-    dip_out[...] = vecs[X] + alpha * (vecs[U] + beta * vecs[PP])
-    res_out[...] = vecs[R] - alpha * (vecs[W] + beta * vecs[S])
 
 
 def per_device(n, positions, field, inv_polar, x_spline, yz_spline, tile_list, tile_count):
@@ -503,11 +518,11 @@
     square = pltpu.VMEM((GRID, GRID), F32)
     sem = pltpu.SemaphoreType.DMA
     out = jax.ShapeDtypeStruct((3, atoms), F32)
-    return pl.pallas_call(
+    dip_a, dip_b, res_a, res_b, step = pl.pallas_call(
         functools.partial(solve_kernel, n),
-        out_shape=(out, out),
+        out_shape=(out,) * 5,
         in_specs=[sm, sm] + [vm] * 9,
-        out_specs=(vm, vm),
+        out_specs=(vm,) * 5,
         scratch_shapes=[
             pltpu.SMEM((blocks, 2 * HALO_BLK + 1), F32),
             pltpu.VMEM((blocks + 2 * HALO_BLK, 8, TILE), F32),
@@ -518,14 +533,15 @@
             pltpu.VMEM((GRID, atoms), F32),
             pltpu.VMEM((GRID, atoms), F32),
             pltpu.VMEM((2 * atoms, 2 * GRID), BF16),
-            pltpu.VMEM((3 * GRID, 2 * atoms), BF16),
+            pltpu.VMEM((4 * GRID, 2 * atoms), BF16),
             pltpu.VMEM((2 * GRID, 2 * atoms), BF16),
             pltpu.VMEM((2 * GRID, 2 * atoms), BF16),
             pltpu.VMEM((4, GRID, GRID), F32),
             pltpu.VMEM((4, GRID, GRID), F32),
             square,
+            square,
             pltpu.VMEM((4, GRID, GRID), F32),
-            pltpu.VMEM((ORDER * GRID, 3 * GRID), BF16),
+            pltpu.VMEM((ORDER * GRID, 4 * GRID), BF16),
             square,
             square, square, square, square,
             square, square, square, square,
@@ -533,8 +549,8 @@
             pltpu.VMEM((nz, 8, TILE), F32),
             pltpu.VMEM((8, TILE), F32),
             pltpu.VMEM((nq, 8, TILE), F32),
-            pltpu.VMEM((9, 3, atoms), F32),
-            pltpu.VMEM((3, 8, TILE), F32),
+            pltpu.VMEM((5, 3, atoms), F32),
+            pltpu.VMEM((2, 8, TILE), F32),
             sem((2,)), sem((2,)),
             sem((4,)), sem((4,)),
             sem((4,)), sem((4,)),
@@ -548,8 +564,9 @@
         compiler_params=pltpu.CompilerParams(
             collective_id=0, has_side_effects=True, vmem_limit_bytes=56 * 1024 * 1024
         ),
-    )(tile_list, tile_count, positions, field, inv_polar.reshape(1, atoms), x_spline, yz_spline,
+    )(tile_list, tile_count, positions, field, inv_polar.reshape(1, atoms), x_spline.transpose(1, 0, 2), yz_spline,
       four, four_t, four_x, four_xt)
+    return dip_a + step * dip_b, res_a - step * res_b
 
 
 def solution(mesh):

time: 156 us -> 145 us (0.929)
  Pallas kernels: 151 us -> 143 us
  local copies, waits for them, and re-layouts: 4.07 us -> 0 us
    pallas_call x1, Pallas kernels: 151 us -> 143 us  [per_device(): pl.pallas_call(functools.partial(solve_kernel, n), out_shape=(out,) * 5,...]
    unnamed x3 -> x0, local copies, waits for them, and re-layouts: 4.07 us -> none
where the time goes in v2:
time: 145 us
  Pallas kernels  143 us (99%)
    pallas_call x1, Pallas kernels, per_device(): pl.pallas_call(functools.partial(solve_kernel, n), out_shape=(out,) * 5,...  143 us

profile of v2, /device:TPU:33, one launch (start us, length us, event | category | flops | bytes accessed | tf_op | source)
XLA Modules:
  0.0 144.6 jit_solution(4761567834761281340)
XLA Ops:
  0.6 142.5 %shard_map.122 = (f32[3,1024]{1,0:T(4,128)}, f32[3,1024]{1,0:T(4,128)}, f32[3,1024]{1,0:T(4,128)}, f32[3,1024]{1,0:T(4,128)}, f32[3,1024]{1,0:T(4,128)}) custom-call(s32[8,7]{1,0:T(8,128)} %tile_list.1, s32[8]{0:T(128)} %tile_count.1, f32[3,1024]{1,0:T(4,128)} %pos.1, f32[3,1024]{1,0:T(4,128)} %field.1, f32[1,1024]{1,0:T(1,128)} %bitcast.3, ...), custom_call_target="tpu_custom_call" | custom-call | tf_op jit(solution)/shard_map/pallas_call | solution.py:521
  143.1 1.4 multiply_subtract_fusion

commit v3 on v2

--- a/solution.py
+++ b/solution.py
@@ -16,7 +16,6 @@
 PAIR_C = 0.025
 RECIP_C = 8192.0
 DAMP = 0.0008
-EXACT = lax.Precision.HIGHEST
 MESH = pl.DeviceIdType.MESH
 F32 = jnp.float32
 BF16 = jnp.bfloat16
@@ -42,8 +41,14 @@
     return hi, (x - hi.astype(F32)).astype(BF16)
 
 
-def exact_dot(a, b):
-    return jnp.dot(a, b, precision=EXACT, preferred_element_type=F32)
+def left_dot(stacked, x):
+    hi, lo = split(x)
+    return fast_dot(stacked[...], jnp.concatenate([hi, hi, lo], axis=0))
+
+
+def right_dot(x, stacked):
+    hi, lo = split(x)
+    return fast_dot(jnp.concatenate([hi, lo, hi], axis=1), stacked[...])
 
 
 def fast_dot(a, b):
@@ -65,16 +70,20 @@
     field,
     inv_polar,
     x_spline,
-    yz,
-    four,
-    four_t,
-    four_x,
-    four_xt,
+    yz_hbm,
+    fwd_right,
+    fwd_left,
+    x_left,
+    xt_left,
+    inv_left,
+    inv_right,
     dip_a,
     dip_b,
     res_a,
     res_b,
     step_out,
+    yz,
+    yz_sem,
     link,
     ext,
     home,
@@ -84,7 +93,7 @@
     y_t,
     dy_t,
     zz,
-    zt4,
+    zt3,
     lhs_hi,
     lhs_lo,
     rim,
@@ -92,7 +101,7 @@
     own_plane,
     pot,
     pot_in,
-    pot4,
+    pot3,
     green,
     f1_src,
     f1_dst,
@@ -158,6 +167,9 @@
     def rows(i, size):
         return pl.ds(pl.multiple_of(i * size, size), size)
 
+    yz_copy = pltpu.make_async_copy(yz_hbm, yz, yz_sem)
+    yz_copy.start()
+
     barrier = pltpu.get_barrier_semaphore()
     for d in far_first(nz):
         pl.semaphore_signal(barrier, inc=1, device_id={"gx": z_peer(d)[1]}, device_id_type=MESH)
@@ -183,10 +195,9 @@
         for part in range(2):
             at_rows = pl.ds(pl.multiple_of(part * atoms + b * TILE, TILE), TILE)
             hi, lo = split(yz[2 + part, cols, :].T)
-            zt4[:GRID, at_rows] = hi
-            zt4[GRID : 2 * GRID, at_rows] = hi
-            zt4[2 * GRID : 3 * GRID, at_rows] = lo
-            zt4[3 * GRID :, at_rows] = lo
+            zt3[:GRID, at_rows] = hi
+            zt3[GRID : 2 * GRID, at_rows] = hi
+            zt3[2 * GRID :, at_rows] = lo
         here = pos[:, cols]
         for c in range(3):
             home[c, cols, :] = jnp.broadcast_to(here[c : c + 1], (TILE, TILE)).T
@@ -300,8 +311,8 @@
             lhs_hi[band, atoms:] = hi
             lhs_lo[band, atoms:] = lo
         size = len(planes) * GRID
-        wide = fast_dot(lhs_hi[:size, :], zz[...]) + fast_dot(lhs_lo[:size, :], zz[...])
-        return wide[:, :GRID] + wide[:, GRID:]
+        wide = fast_dot(lhs_hi[:size, :], zz[...])
+        return wide[:, :GRID] + wide[:, GRID:] + fast_dot(lhs_lo[:size, :], zz[:, :GRID])
 
     chunk = 32
 
@@ -340,32 +351,39 @@
             near[c : c + 1, cols] = jnp.sum(pair_acc[c, cols, :].T, axis=0, keepdims=True)
         return carry
 
-    def gather_chunk(g, carry):
+    arrival = (2,) + tuple(2 - OFFSETS[k] for k in (2, 3, 0, 1))
+
+    def gather(first, last):
         wide = 256
-        cols = rows(g, wide)
-        plain = fast_dot(pot4[...], zt4[:, cols])
-        sa = jnp.zeros((GRID, wide), F32)
-        sb = sa
-        for p in range(ORDER):
-            band = plain[p * GRID : (p + 1) * GRID]
-            sa = sa + x_spline[p, 1:2, cols] * band
-            sb = sb + x_spline[p, 0:1, cols] * band
-        far[0:1, cols] = jnp.sum(sa * y_t[:, cols], axis=0, keepdims=True)
-        far[1:2, cols] = jnp.sum(sb * dy_t[:, cols], axis=0, keepdims=True)
-        tilted = fast_dot(pot4[...], zt4[:, pl.ds(pl.multiple_of(atoms + g * wide, wide), wide)])
-        sc = jnp.zeros((GRID, wide), F32)
-        for p in range(ORDER):
-            sc = sc + x_spline[p, 0:1, cols] * tilted[p * GRID : (p + 1) * GRID]
-        far[2:3, cols] = jnp.sum(sc * y_t[:, cols], axis=0, keepdims=True)
-        return carry
+        band = slice(first * GRID, last * GRID)
+
+        def chunk_of(g, carry):
+            cols = rows(g, wide)
+            tilt_cols = pl.ds(pl.multiple_of(atoms + g * wide, wide), wide)
+            plain = fast_dot(pot3[band, :], zt3[:, cols])
+            tilted = fast_dot(pot3[band, :], zt3[:, tilt_cols])
+            sa = jnp.zeros((GRID, wide), F32)
+            sb, sc = sa, sa
+            for slot, p in enumerate(arrival[first:last]):
+                here = slice(slot * GRID, (slot + 1) * GRID)
+                value = x_spline[p, 0:1, cols]
+                sa = sa + x_spline[p, 1:2, cols] * plain[here]
+                sb = sb + value * plain[here]
+                sc = sc + value * tilted[here]
+            for c, part in enumerate((sa * y_t[:, cols], sb * dy_t[:, cols], sc * y_t[:, cols])):
+                total = jnp.sum(part, axis=0, keepdims=True)
+                far[c : c + 1, cols] = total if first == 0 else far[c : c + 1, cols] + total
+            return carry
+
+        lax.fori_loop(0, atoms // wide, chunk_of, 0)
 
     def put_plane(p, plane):
         hi, lo = split(plane)
-        band = slice(p * GRID, (p + 1) * GRID)
-        pot4[band, :GRID] = hi
-        pot4[band, GRID : 2 * GRID] = lo
-        pot4[band, 2 * GRID : 3 * GRID] = hi
-        pot4[band, 3 * GRID :] = lo
+        at = arrival.index(p)
+        band = slice(at * GRID, (at + 1) * GRID)
+        pot3[band, :GRID] = hi
+        pot3[band, GRID : 2 * GRID] = lo
+        pot3[band, 2 * GRID :] = hi
 
     def put_vector():
         v = vecs[U]
@@ -377,6 +395,7 @@
         for slot, k in enumerate(pair):
             rim[k] = both[slot * GRID : (slot + 1) * GRID]
 
+    yz_copy.wait()
     lax.fori_loop(0, blocks, prepare, 0)
     vecs[R] = field[...]
     vecs[U] = field[...] / ip
@@ -387,28 +406,24 @@
     put_vector()
     spread_pair((0, 1))
     spread_pair((2, 3))
+    own_plane[...] = spread([2])
+    lax.fori_loop(0, blocks, prepare_more, 0)
+    prepare_green()
     pl.semaphore_wait(barrier, (nz - 1) + (nq - 1) + len(OFFSETS))
     for k in range(len(OFFSETS)):
         rim_copy(k).start()
     for c in vec_copies():
         c.start()
-    own_plane[...] = spread([2])
 
     def sweep(it, carry):
         own = own_plane[...]
         for k in range(len(OFFSETS)):
             rim_copy(k).wait_recv()
             own = own + rim_in[k]
-        along_z = exact_dot(own, four_t[...])
-        f1_src[...] = exact_dot(four[...], along_z)
+        f1_src[...] = left_dot(fwd_left, right_dot(own, fwd_right))
         for c in f1_copies():
             c.start()
         f1_dst[rows(my_q, nz), :] = f1_src[rows(my_q, nz), :]
-
-        @pl.when(it == 0)
-        def _():
-            lax.fori_loop(0, blocks, prepare_more, 0)
-            prepare_green()
 
         for c in vec_copies():
             c.wait_recv()
@@ -426,9 +441,9 @@
 
         for c in f2_copies():
             c.wait_recv()
-        lines = exact_dot(four_x[...], f2_dst[...])
+        lines = left_dot(x_left, f2_dst[...])
         scaled = lines * green[...]
-        a_src[...] = exact_dot(four_xt[...], scaled)
+        a_src[...] = left_dot(xt_left, scaled)
         for c in a_copies():
             c.start()
         a_dst[rows(my_z, nq), :] = a_src[rows(my_z, nq), :]
@@ -443,8 +458,7 @@
         reduce_middle()
         for c in b_copies():
             c.wait_recv()
-        along_k = exact_dot(four_t[...], b_dst[...])
-        mine = exact_dot(along_k, four[...])
+        mine = right_dot(left_dot(inv_left, b_dst[...]), inv_right)
         pot[...] = mine
         for k in (2, 3, 0, 1):
             pot_copy(k).start()
@@ -454,10 +468,14 @@
                 c.wait_send()
         for k in range(len(OFFSETS)):
             rim_copy(k).wait_send()
-        for k in (2, 3, 0, 1):
+        for k in (2, 3):
             pot_copy(k).wait_recv()
             put_plane(2 - OFFSETS[k], pot_in[k])
-        lax.fori_loop(0, atoms // 256, gather_chunk, 0)
+        gather(0, 3)
+        for k in (0, 1):
+            pot_copy(k).wait_recv()
+            put_plane(2 - OFFSETS[k], pot_in[k])
+        gather(3, ORDER)
         u = vecs[U]
         image = ip * u + far[...] - PAIR_C * (near[...] - u)
         gamma, delta = reduce_end()
@@ -509,10 +527,22 @@
     q, z = rows_x % nq, rows_x // nq
     plane = (q // NC) * (nz * NC) + z * NC + q % NC
     table = basis(GRID)
-    four = jnp.asarray(table, F32)
-    four_t = jnp.asarray(table.T.copy(), F32)
-    four_x = jnp.asarray(table[:, plane], F32)
-    four_xt = jnp.asarray(table[:, plane].T.copy(), F32)
+    across = table[:, plane]
+
+    def parts(t):
+        whole = jnp.asarray(t, F32)
+        return split(whole)
+
+    def left_of(t):
+        hi, lo = parts(t)
+        return jnp.concatenate([hi, lo, hi], axis=1)
+
+    def right_of(t):
+        hi, lo = parts(t)
+        return jnp.concatenate([hi, hi, lo], axis=0)
+
+    with jax.ensure_compile_time_eval():
+        tables = (right_of(table.T), left_of(table), left_of(across), left_of(across.T), left_of(table.T), right_of(table))
     vm = pl.BlockSpec(memory_space=pltpu.VMEM)
     sm = pl.BlockSpec(memory_space=pltpu.SMEM)
     square = pltpu.VMEM((GRID, GRID), F32)
@@ -521,9 +551,11 @@
     dip_a, dip_b, res_a, res_b, step = pl.pallas_call(
         functools.partial(solve_kernel, n),
         out_shape=(out,) * 5,
-        in_specs=[sm, sm] + [vm] * 9,
+        in_specs=[sm, sm] + [vm] * 4 + [pl.BlockSpec(memory_space=pl.ANY)] + [vm] * 6,
         out_specs=(vm,) * 5,
         scratch_shapes=[
+            pltpu.VMEM(yz_spline.shape, F32),
+            sem,
             pltpu.SMEM((blocks, 2 * HALO_BLK + 1), F32),
             pltpu.VMEM((blocks + 2 * HALO_BLK, 8, TILE), F32),
             pltpu.VMEM((3, atoms, TILE), F32),
@@ -533,7 +565,7 @@
             pltpu.VMEM((GRID, atoms), F32),
             pltpu.VMEM((GRID, atoms), F32),
             pltpu.VMEM((2 * atoms, 2 * GRID), BF16),
-            pltpu.VMEM((4 * GRID, 2 * atoms), BF16),
+            pltpu.VMEM((3 * GRID, 2 * atoms), BF16),
             pltpu.VMEM((2 * GRID, 2 * atoms), BF16),
             pltpu.VMEM((2 * GRID, 2 * atoms), BF16),
             pltpu.VMEM((4, GRID, GRID), F32),
@@ -541,7 +573,7 @@
             square,
             square,
             pltpu.VMEM((4, GRID, GRID), F32),
-            pltpu.VMEM((ORDER * GRID, 4 * GRID), BF16),
+            pltpu.VMEM((ORDER * GRID, 3 * GRID), BF16),
             square,
             square, square, square, square,
             square, square, square, square,
@@ -565,7 +597,7 @@
             collective_id=0, has_side_effects=True, vmem_limit_bytes=56 * 1024 * 1024
         ),
     )(tile_list, tile_count, positions, field, inv_polar.reshape(1, atoms), x_spline.transpose(1, 0, 2), yz_spline,
-      four, four_t, four_x, four_xt)
+      *tables)
     return dip_a + step * dip_b, res_a - step * res_b
 
 

time: 145 us -> 143 us (0.986)
  Pallas kernels: 143 us -> 141 us
where the time goes in v3:
time: 143 us
  Pallas kernels  141 us (99%)
    pallas_call x1, Pallas kernels, per_device(): pl.pallas_call(functools.partial(solve_kernel, n), out_shape=(out,) * 5,...  141 us

profile of v3, /device:TPU:33, one launch (start us, length us, event | category | flops | bytes accessed | tf_op | source)
XLA Modules:
  0.0 143.2 jit_solution(6185547284575195144)
XLA Ops:
  0.6 141.2 %shard_map.140 = (f32[3,1024]{1,0:T(4,128)}, f32[3,1024]{1,0:T(4,128)}, f32[3,1024]{1,0:T(4,128)}, f32[3,1024]{1,0:T(4,128)}, f32[3,1024]{1,0:T(4,128)}) custom-call(s32[8,7]{1,0:T(8,128)} %tile_list.1, s32[8]{0:T(128)} %tile_count.1, f32[3,1024]{1,0:T(4,128)} %pos.1, f32[3,1024]{1,0:T(4,128)} %field.1, f32[1,1024]{1,0:T(1,128)} %bitcast.3, ...), custom_call_target="tpu_custom_call" | custom-call | tf_op jit(solution)/shard_map/pallas_call | solution.py:551
  141.8 1.4 multiply_subtract_fusion

commit v4 on v3

--- a/solution.py
+++ b/solution.py
@@ -73,8 +73,6 @@
     yz_hbm,
     fwd_right,
     fwd_left,
-    x_left,
-    xt_left,
     inv_left,
     inv_right,
     dip_a,
@@ -103,14 +101,10 @@
     pot_in,
     pot3,
     green,
-    f1_src,
-    f1_dst,
-    f2_src,
-    f2_dst,
+    f_src,
+    f_dst,
     a_src,
     a_dst,
-    b_src,
-    b_dst,
     ra_src,
     ra_dst,
     rb_src,
@@ -123,14 +117,10 @@
     c_rs,
     h_ss,
     h_rs,
-    f1_ss,
-    f1_rs,
-    f2_ss,
-    f2_rs,
+    f_ss,
+    f_rs,
     a_ss,
     a_rs,
-    b_ss,
-    b_rs,
     ra_ss,
     ra_rs,
     rb_ss,
@@ -171,12 +161,22 @@
     yz_copy.start()
 
     barrier = pltpu.get_barrier_semaphore()
-    for d in far_first(nz):
-        pl.semaphore_signal(barrier, inc=1, device_id={"gx": z_peer(d)[1]}, device_id_type=MESH)
-    for d in far_first(nq):
-        pl.semaphore_signal(barrier, inc=1, device_id={"gx": q_peer(d)[1]}, device_id_type=MESH)
-    for d in OFFSETS:
-        pl.semaphore_signal(barrier, inc=1, device_id={"gx": to(d)}, device_id_type=MESH)
+    def greet(peer):
+        pl.semaphore_signal(barrier, inc=1, device_id={"gx": peer}, device_id_type=MESH)
+
+    def every_peer(visit):
+        def ring(i, carry):
+            half = (i + 1) // 2
+            z = (my_z + nz // 2 + jnp.where(i % 2 == 1, -half, half) + nz) % nz
+            for d in range(nq):
+                visit(at((my_q + d) % nq, z))
+            return carry
+
+        lax.fori_loop(0, nz - 1, ring, 0)
+        for d in far_first(nq):
+            visit(q_peer(d)[1])
+
+    every_peer(greet)
 
     def prepare(b, carry):
         cols = rows(b, TILE)
@@ -214,7 +214,7 @@
         col_freq = lax.broadcasted_iota(jnp.int32, (GRID, GRID), 1)
         kx, wx = mode_of(row_freq, GRID)
         kz, wz = mode_of(col_freq, GRID)
-        ky, wy = mode_of(jnp.full((GRID, GRID), my_q * nz + my_z, jnp.int32), GRID)
+        ky, wy = mode_of(jnp.full((GRID, GRID), me, jnp.int32), GRID)
         mode_sq = kx * kx + ky * ky + kz * kz
         safe_sq = jnp.where(mode_sq > 0, mode_sq, 1.0)
         green[...] = jnp.where(mode_sq > 0, RECIP_C * jnp.exp(-DAMP * safe_sq) / safe_sq, 0.0) * wx * wy * wz
@@ -270,33 +270,15 @@
     def pot_copy(k):
         return copy(pot, pot_in.at[k], h_ss.at[k], h_rs.at[k], to(OFFSETS[k]))
 
-    def f1_copies():
-        out = []
-        for d in far_first(nq):
-            q, peer = q_peer(d)
-            out.append(copy(f1_src.at[rows(q, nz)], f1_dst.at[rows(my_q, nz)], f1_ss.at[d], f1_rs.at[d], peer))
-        return out
-
-    def f2_copies():
-        out = []
-        for d in far_first(nz):
-            z, peer = z_peer(d)
-            out.append(copy(f2_src.at[rows(z, nq)], f2_dst.at[rows(my_z, nq)], f2_ss.at[d], f2_rs.at[d], peer))
-        return out
-
-    def a_copies():
-        out = []
-        for d in far_first(nz):
-            z, peer = z_peer(d)
-            out.append(copy(a_src.at[rows(z, nq)], a_dst.at[rows(my_z, nq)], a_ss.at[d], a_rs.at[d], peer))
-        return out
-
-    def b_copies():
-        out = []
-        for d in far_first(nq):
-            q, peer = q_peer(d)
-            out.append(copy(b_src.at[rows(q, nz)], b_dst.at[rows(my_q, nz)], b_ss.at[d], b_rs.at[d], peer))
-        return out
+    def row(i):
+        return pl.ds(i, 1)
+
+    def exchange_start(src, dst, ss, rs):
+        every_peer(lambda peer: copy(src.at[row(peer)], dst.at[row(me)], ss, rs, peer).start())
+        dst[row(me), :] = src[row(me), :]
+
+    def exchange_all(src, dst, ss, rs):
+        return copy(src.at[pl.ds(0, n - 1)], dst.at[pl.ds(0, n - 1)], ss, rs, to(1))
 
     def spread(planes):
         v = vecs[U]
@@ -409,7 +391,7 @@
     own_plane[...] = spread([2])
     lax.fori_loop(0, blocks, prepare_more, 0)
     prepare_green()
-    pl.semaphore_wait(barrier, (nz - 1) + (nq - 1) + len(OFFSETS))
+    pl.semaphore_wait(barrier, n - 1)
     for k in range(len(OFFSETS)):
         rim_copy(k).start()
     for c in vec_copies():
@@ -420,52 +402,30 @@
         for k in range(len(OFFSETS)):
             rim_copy(k).wait_recv()
             own = own + rim_in[k]
-        f1_src[...] = left_dot(fwd_left, right_dot(own, fwd_right))
-        for c in f1_copies():
-            c.start()
-        f1_dst[rows(my_q, nz), :] = f1_src[rows(my_q, nz), :]
+        f_src[...] = left_dot(fwd_left, right_dot(own, fwd_right))
+        exchange_start(f_src, f_dst, f_ss, f_rs)
 
         for c in vec_copies():
             c.wait_recv()
-        lax.fori_loop(0, 2, pair_block, 0)
-
-        for c in f1_copies():
-            c.wait_recv()
-        for z in range(nz):
-            f2_src[z * nq : (z + 1) * nq, :] = f1_dst[pl.ds(z, nq, stride=nz), :]
-        for c in f2_copies():
-            c.start()
-        f2_dst[rows(my_z, nq), :] = f2_src[rows(my_z, nq), :]
-
-        lax.fori_loop(2, blocks, pair_block, 0)
-
-        for c in f2_copies():
-            c.wait_recv()
-        lines = left_dot(x_left, f2_dst[...])
+        lax.fori_loop(0, blocks, pair_block, 0)
+
+        exchange_all(f_src, f_dst, f_ss, f_rs).wait_recv()
+        lines = left_dot(fwd_left, f_dst[...])
         scaled = lines * green[...]
-        a_src[...] = left_dot(xt_left, scaled)
-        for c in a_copies():
-            c.start()
-        a_dst[rows(my_z, nq), :] = a_src[rows(my_z, nq), :]
+        a_src[...] = left_dot(inv_left, scaled)
+        exchange_start(a_src, a_dst, a_ss, a_rs)
         reduce_start(jnp.sum(lines * scaled, axis=0, keepdims=True))
-        for c in a_copies():
-            c.wait_recv()
-        for q in range(nq):
-            b_src[q * nz : (q + 1) * nz, :] = a_dst[pl.ds(q, nz, stride=nq), :]
-        for c in b_copies():
-            c.start()
-        b_dst[rows(my_q, nz), :] = b_src[rows(my_q, nz), :]
+        exchange_all(a_src, a_dst, a_ss, a_rs).wait_recv()
         reduce_middle()
-        for c in b_copies():
-            c.wait_recv()
-        mine = right_dot(left_dot(inv_left, b_dst[...]), inv_right)
+        mine = right_dot(left_dot(inv_left, a_dst[...]), inv_right)
         pot[...] = mine
         for k in (2, 3, 0, 1):
             pot_copy(k).start()
         put_plane(2, mine)
-        for group in (vec_copies(), f1_copies(), f2_copies(), a_copies(), b_copies()):
-            for c in group:
-                c.wait_send()
+        for c in vec_copies():
+            c.wait_send()
+        exchange_all(f_src, f_dst, f_ss, f_rs).wait_send()
+        exchange_all(a_src, a_dst, a_ss, a_rs).wait_send()
         for k in range(len(OFFSETS)):
             rim_copy(k).wait_send()
         for k in (2, 3):
@@ -523,11 +483,7 @@
     blocks = atoms // TILE
     nq = NX * NC
     nz = n // nq
-    rows_x = np.arange(GRID)
-    q, z = rows_x % nq, rows_x // nq
-    plane = (q // NC) * (nz * NC) + z * NC + q % NC
     table = basis(GRID)
-    across = table[:, plane]
 
     def parts(t):
         whole = jnp.asarray(t, F32)
@@ -542,7 +498,7 @@
         return jnp.concatenate([hi, hi, lo], axis=0)
 
     with jax.ensure_compile_time_eval():
-        tables = (right_of(table.T), left_of(table), left_of(across), left_of(across.T), left_of(table.T), right_of(table))
+        tables = (right_of(table.T), left_of(table), left_of(table.T), right_of(table))
     vm = pl.BlockSpec(memory_space=pltpu.VMEM)
     sm = pl.BlockSpec(memory_space=pltpu.SMEM)
     square = pltpu.VMEM((GRID, GRID), F32)
@@ -551,7 +507,7 @@
     dip_a, dip_b, res_a, res_b, step = pl.pallas_call(
         functools.partial(solve_kernel, n),
         out_shape=(out,) * 5,
-        in_specs=[sm, sm] + [vm] * 4 + [pl.BlockSpec(memory_space=pl.ANY)] + [vm] * 6,
+        in_specs=[sm, sm] + [vm] * 4 + [pl.BlockSpec(memory_space=pl.ANY)] + [vm] * 4,
         out_specs=(vm,) * 5,
         scratch_shapes=[
             pltpu.VMEM(yz_spline.shape, F32),
@@ -576,7 +532,6 @@
             pltpu.VMEM((ORDER * GRID, 3 * GRID), BF16),
             square,
             square, square, square, square,
-            square, square, square, square,
             pltpu.VMEM((8, TILE), F32),
             pltpu.VMEM((nz, 8, TILE), F32),
             pltpu.VMEM((8, TILE), F32),
@@ -586,10 +541,7 @@
             sem((2,)), sem((2,)),
             sem((4,)), sem((4,)),
             sem((4,)), sem((4,)),
-            sem((nq,)), sem((nq,)),
-            sem((nz,)), sem((nz,)),
-            sem((nz,)), sem((nz,)),
-            sem((nq,)), sem((nq,)),
+            sem, sem, sem, sem,
             sem((nz,)), sem((nz,)),
             sem((nq,)), sem((nq,)),
         ],

time: 143 us -> 134 us (0.937)
  Pallas kernels: 141 us -> 132 us
    pallas_call x1, Pallas kernels: 141 us -> 132 us  [per_device(): pl.pallas_call(functools.partial(solve_kernel, n), out_shape=(out,) * 5,...]
where the time goes in v4:
time: 134 us
  Pallas kernels  132 us (99%)
  other arithmetic  1.41 us (1%)
    pallas_call x1, Pallas kernels, per_device(): pl.pallas_call(functools.partial(solve_kernel, n), out_shape=(out,) * 5,...  132 us

profile of v4, /device:TPU:33, one launch (start us, length us, event | category | flops | bytes accessed | tf_op | source)
XLA Modules:
  0.0 134.1 jit_solution(208322865413311870)
XLA Ops:
  0.6 132.0 %shard_map.122 = (f32[3,1024]{1,0:T(4,128)}, f32[3,1024]{1,0:T(4,128)}, f32[3,1024]{1,0:T(4,128)}, f32[3,1024]{1,0:T(4,128)}, f32[3,1024]{1,0:T(4,128)}) custom-call(s32[8,7]{1,0:T(8,128)} %tile_list.1, s32[8]{0:T(128)} %tile_count.1, f32[3,1024]{1,0:T(4,128)} %pos.1, f32[3,1024]{1,0:T(4,128)} %field.1, f32[1,1024]{1,0:T(1,128)} %bitcast.3, ...), custom_call_target="tpu_custom_call" | custom-call | tf_op jit(solution)/shard_map/pallas_call | solution.py:507
  132.7 1.4 %multiply_subtract_fusion = (f32[3,1024]{1,0:T(4,128)}, f32[3,1024]{1,0:T(4,128)}) fusion(f32[3,1024]{1,0:T(4,128)} %get-tuple-element.10, f32[3,1024]{1,0:T(4,128)} %get-tuple-element.8, f32[3,1024]{1,0:T(4,128)} %get-tuple-element.11, f32[3,1024]{1,0:T(4,128)} %get-tuple-element.7, f32[3,1024]{1,0:T(4,128)} %get-tuple-element.9), kind=kLoop, calls=%fused_computation | loop fusion | flops 12288 | bytes 86016 | tf_op jit(solution)/shard_map/sub | solution.py:553

commit v5 on v4

--- a/solution.py
+++ b/solution.py
@@ -168,7 +168,7 @@
         def ring(i, carry):
             half = (i + 1) // 2
             z = (my_z + nz // 2 + jnp.where(i % 2 == 1, -half, half) + nz) % nz
-            for d in range(nq):
+            for d in far_first(nq) + [0]:
                 visit(at((my_q + d) % nq, z))
             return carry
 
@@ -280,21 +280,19 @@
     def exchange_all(src, dst, ss, rs):
         return copy(src.at[pl.ds(0, n - 1)], dst.at[pl.ds(0, n - 1)], ss, rs, to(1))
 
-    def spread(planes):
+    def spread(p, slot):
         v = vecs[U]
-        for slot, p in enumerate(planes):
-            value = x_spline[p, 0:1, :]
-            slope = x_spline[p, 1:2, :]
-            band = slice(slot * GRID, (slot + 1) * GRID)
-            hi, lo = split(y_t[...] * (v[0:1] * slope) + dy_t[...] * (v[1:2] * value))
-            lhs_hi[band, :atoms] = hi
-            lhs_lo[band, :atoms] = lo
-            hi, lo = split(y_t[...] * (v[2:3] * value))
-            lhs_hi[band, atoms:] = hi
-            lhs_lo[band, atoms:] = lo
-        size = len(planes) * GRID
-        wide = fast_dot(lhs_hi[:size, :], zz[...])
-        return wide[:, :GRID] + wide[:, GRID:] + fast_dot(lhs_lo[:size, :], zz[:, :GRID])
+        value = x_spline[p, 0:1, :]
+        slope = x_spline[p, 1:2, :]
+        band = slice(slot * GRID, (slot + 1) * GRID)
+        hi, lo = split(y_t[...] * (v[0:1] * slope) + dy_t[...] * (v[1:2] * value))
+        lhs_hi[band, :atoms] = hi
+        lhs_lo[band, :atoms] = lo
+        hi, lo = split(y_t[...] * (v[2:3] * value))
+        lhs_hi[band, atoms:] = hi
+        lhs_lo[band, atoms:] = lo
+        wide = fast_dot(lhs_hi[band, :], zz[...])
+        return wide[:, :GRID] + wide[:, GRID:] + fast_dot(lhs_lo[band, :], zz[:, :GRID])
 
     chunk = 32
 
@@ -372,10 +370,8 @@
         for b in range(blocks):
             ext[HALO_BLK + b, 0:3, :] = v[:, b * TILE : (b + 1) * TILE]
 
-    def spread_pair(pair):
-        both = spread([OFFSETS[k] + 2 for k in pair])
-        for slot, k in enumerate(pair):
-            rim[k] = both[slot * GRID : (slot + 1) * GRID]
+    def spread_rim(k):
+        rim[k] = spread(OFFSETS[k] + 2, k % 2)
 
     yz_copy.wait()
     lax.fori_loop(0, blocks, prepare, 0)
@@ -386,9 +382,9 @@
     scal[...] = jnp.ones_like(scal)
     ra_src[...] = jnp.zeros_like(ra_src)
     put_vector()
-    spread_pair((0, 1))
-    spread_pair((2, 3))
-    own_plane[...] = spread([2])
+    for k in range(len(OFFSETS)):
+        spread_rim(k)
+    own_plane[...] = spread(2, 0)
     lax.fori_loop(0, blocks, prepare_more, 0)
     prepare_green()
     pl.semaphore_wait(barrier, n - 1)
@@ -452,16 +448,15 @@
         def _():
             residual = vecs[R] - alpha * new_s
             vecs[U] = residual / ip
+            for k in range(len(OFFSETS)):
+                spread_rim(k)
+                rim_copy(k).start()
             put_vector()
             for c in vec_copies():
                 c.start()
+            own_plane[...] = spread(2, 0)
             vecs[R] = residual
             vecs[X] = vecs[X] + alpha * new_p
-            for pair in ((0, 1), (2, 3)):
-                spread_pair(pair)
-                for k in pair:
-                    rim_copy(k).start()
-            own_plane[...] = spread([2])
 
         @pl.when(it == ITERS - 1)
         def _():

time: 134 us -> 134 us (level)
  no operation moved by 1% of the time
where the time goes in v5:
time: 134 us
  Pallas kernels  132 us (99%)
  other arithmetic  1.41 us (1%)
    pallas_call x1, Pallas kernels, per_device(): pl.pallas_call(functools.partial(solve_kernel, n), out_shape=(out,) * 5,...  132 us

profile of v5, /device:TPU:33, one launch (start us, length us, event | category | flops | bytes accessed | tf_op | source)
XLA Modules:
  0.0 134.1 jit_solution(1663147814947439088)
XLA Ops:
  0.6 132.0 %shard_map.122 = (f32[3,1024]{1,0:T(4,128)}, f32[3,1024]{1,0:T(4,128)}, f32[3,1024]{1,0:T(4,128)}, f32[3,1024]{1,0:T(4,128)}, f32[3,1024]{1,0:T(4,128)}) custom-call(s32[8,7]{1,0:T(8,128)} %tile_list.1, s32[8]{0:T(128)} %tile_count.1, f32[3,1024]{1,0:T(4,128)} %pos.1, f32[3,1024]{1,0:T(4,128)} %field.1, f32[1,1024]{1,0:T(1,128)} %bitcast.3, ...), custom_call_target="tpu_custom_call" | custom-call | tf_op jit(solution)/shard_map/pallas_call | solution.py:502
  132.7 1.4 %multiply_subtract_fusion = (f32[3,1024]{1,0:T(4,128)}, f32[3,1024]{1,0:T(4,128)}) fusion(f32[3,1024]{1,0:T(4,128)} %get-tuple-element.10, f32[3,1024]{1,0:T(4,128)} %get-tuple-element.8, f32[3,1024]{1,0:T(4,128)} %get-tuple-element.11, f32[3,1024]{1,0:T(4,128)} %get-tuple-element.7, f32[3,1024]{1,0:T(4,128)} %get-tuple-element.9), kind=kLoop, calls=%fused_computation | loop fusion | flops 12288 | bytes 86016 | tf_op jit(solution)/shard_map/sub | solution.py:548
